TPU v7x, 256 devices: a whole 4x4x8 slice. The times are simulated.
256 devices in a mesh: row: 16 (over z, core), col: 16 (over y, x).
Axes of the slice: x: 4, y: 4, z: 8, core: 2. Of those that a mesh axis runs over, the one named last changes fastest.
Arguments:
- velocity: float32 [1, 3, 128, 256, 256], P(None, None, 'row', 'col'), may hold values from -6 to 6
- tendency: float32 [1, 3, 128, 256, 256], P(None, None, 'row', 'col'), may hold values from -6 to 6
- step_size: float32 [1], replicated, may hold values from 0.1 to 0.6
- lift_weight: float32 [32, 3], replicated, may hold values from -3.5 to 3.5
- lift_bias: float32 [32], replicated, may hold values from -3 to 3
- spectral_weight: bfloat16 [2, 32, 32, 32, 1024], P(None, 'row', 'col'), may hold values from -6 to 6
- local_weight: float32 [32, 32], replicated, may hold values from -1 to 1
- local_bias: float32 [32], replicated, may hold values from -3 to 3
Outputs:
- features: bfloat16 [1, 32, 128, 256, 256], P(None, None, 'row', 'col')
All inputs are finite; a program needn't handle non-finite values.
Results may differ from a plain program's by a relative error of at most 0.001.
Values sent between devices are 32-bit elements; how exact they have to be, the bound alone decides.
No kernel may reach another device: no remote copies, remote signals or barrier semaphores. Data moves between devices by JAX's collectives and lax.ppermute only.
A program may use at most 64 MiB of HBM per device.

v0:
```python
import math

import jax
import jax.numpy as jnp
from jax import lax
from jax.sharding import PartitionSpec as P

KX = 32
KY = 32
KZ = 32
NZ = 256


def wavenumbers(count):
    index = jnp.arange(count, dtype=jnp.int32)
    return jnp.where(index < count // 2, index, index - count)


def angles(waves, points, length):
    return jnp.mod(waves[:, None] * points[None, :], length).astype(jnp.float32) * (
        2.0 * math.pi / length
    )


def forward_table(angle):
    cosine = jnp.cos(angle)
    sine = jnp.sin(angle)
    return jnp.stack([jnp.stack([cosine, -sine], 0), jnp.stack([sine, cosine], 0)], 0)


def inverse_table(angle):
    cosine = jnp.cos(angle)
    sine = jnp.sin(angle)
    return jnp.stack([jnp.stack([cosine, sine], 0), jnp.stack([-sine, cosine], 0)], 0)


def per_device(
    velocity, tendency, step_size, lift_weight, lift_bias, spectral_weight, local_weight, local_bias
):
    highest = lax.Precision.HIGHEST
    samples = velocity.shape[0]
    rows_x = velocity.shape[2]
    rows_y = velocity.shape[3]
    channels = lift_weight.shape[0]
    row_count = lax.axis_size("row")
    col_count = lax.axis_size("col")
    full_x = rows_x * row_count
    full_y = rows_y * col_count
    kz_local = KZ // col_count
    ky_local = KY // row_count
    advanced = velocity + step_size[:, None, None, None, None] * tendency
    width_in = advanced.shape[1]
    z_angle = angles(jnp.arange(KZ, dtype=jnp.int32), jnp.arange(NZ, dtype=jnp.int32), NZ)
    z_table = jnp.stack([jnp.cos(z_angle), -jnp.sin(z_angle)], 0).reshape(
        2, col_count, kz_local, NZ
    )
    z_modes = jnp.einsum("bcxyz,rdkz->bcxdrky", advanced, z_table, precision=highest)
    y_angle = angles(wavenumbers(KY), jnp.arange(full_y, dtype=jnp.int32), full_y)
    outgoing = z_modes.reshape(samples, width_in, rows_x, col_count, -1)
    arrived = lax.all_to_all(outgoing, "col", split_axis=3, concat_axis=3, tiled=True)
    arrived = arrived.reshape(samples, width_in, rows_x, col_count, 2, kz_local, rows_y)
    y_table = forward_table(y_angle).reshape(2, 2, row_count, ky_local, col_count, rows_y)
    by_y = jnp.einsum("bcxsrky,rtdlsy->bcdtklx", arrived, y_table, precision=highest)
    by_y = by_y.reshape(samples, width_in, row_count, -1)
    pencils_x = lax.all_to_all(by_y, "row", split_axis=2, concat_axis=2, tiled=True)
    pencils_x = pencils_x.reshape(samples, width_in, row_count, 2, kz_local, ky_local, rows_x)
    x_angle = angles(wavenumbers(KX), jnp.arange(full_x, dtype=jnp.int32), full_x)
    x_table = forward_table(x_angle).reshape(2, 2, KX, row_count, rows_x)
    coeffs = jnp.einsum("bcsrklx,rtasx->bctkal", pencils_x, x_table, precision=highest)
    coeffs = coeffs * (1.0 / (full_x * full_y * NZ))
    part_index = jnp.arange(2, dtype=jnp.int32)[:, None, None, None]
    kz_global = (
        lax.axis_index("col") * kz_local
        + jnp.arange(kz_local, dtype=jnp.int32)[None, :, None, None]
    )
    kx_index = jnp.arange(KX, dtype=jnp.int32)[None, None, :, None]
    ky_global = (
        lax.axis_index("row") * ky_local
        + jnp.arange(ky_local, dtype=jnp.int32)[None, None, None, :]
    )
    zero_mode = ((part_index == 0) & (kz_global == 0) & (kx_index == 0) & (ky_global == 0)).astype(
        jnp.float32
    )
    coeffs = jnp.einsum("ij,bjtkal->bitkal", lift_weight, coeffs, precision=highest)
    coeffs = coeffs + lift_bias[None, :, None, None, None, None] * zero_mode[None, None]
    weights = spectral_weight.astype(jnp.float32).reshape(
        2, ky_local, kz_local, KX, channels, channels
    )

    def mixing(weight_part, data_part):
        return jnp.einsum("lkaoi,bikal->bokal", weight_part, data_part, precision=highest)

    coef_real = coeffs[:, :, 0]
    coef_imag = coeffs[:, :, 1]
    mixed_real = mixing(weights[0], coef_real) - mixing(weights[1], coef_imag)
    mixed_imag = mixing(weights[0], coef_imag) + mixing(weights[1], coef_real)
    mixed = jnp.stack([mixed_real, mixed_imag], 2)
    x_back = inverse_table(x_angle).reshape(2, 2, KX, row_count, rows_x)
    cells_x = jnp.einsum("botkal,tuadx->boduklx", mixed, x_back, precision=highest)
    cells_x = cells_x.reshape(samples, channels, row_count, -1)
    by_cells = lax.all_to_all(cells_x, "row", split_axis=2, concat_axis=2, tiled=True)
    by_cells = by_cells.reshape(samples, channels, row_count, 2, kz_local, ky_local, rows_x)
    y_back_table = inverse_table(y_angle).reshape(2, 2, row_count, ky_local, col_count, rows_y)
    cells_y = jnp.einsum("bosuklx,uvsldy->bodvkxy", by_cells, y_back_table, precision=highest)
    cells_y = cells_y.reshape(samples, channels, col_count, -1)
    pencils_z = lax.all_to_all(cells_y, "col", split_axis=2, concat_axis=2, tiled=True)
    pencils_z = pencils_z.reshape(samples, channels, col_count, 2, kz_local, rows_x, rows_y)
    doubling = jnp.where(jnp.arange(KZ, dtype=jnp.int32) == 0, 1.0, 2.0).astype(jnp.float32)[
        :, None
    ]
    z_back = jnp.stack([doubling * jnp.cos(z_angle), -doubling * jnp.sin(z_angle)], 0).reshape(
        2, col_count, kz_local, NZ
    )
    spectral = jnp.einsum("bodvkxy,vdkz->boxyz", pencils_z, z_back, precision=highest)
    combined = jnp.dot(local_weight, lift_weight, precision=highest)
    offset = jnp.dot(local_weight, lift_bias, precision=highest) + local_bias
    local_term = (
        jnp.einsum("oj,bjxyz->boxyz", combined, advanced, precision=highest)
        + offset[None, :, None, None, None]
    )
    return jax.nn.gelu(spectral + local_term).astype(jnp.bfloat16)


def solution(mesh):
    in_specs = (
        P(None, None, "row", "col", None),
        P(None, None, "row", "col", None),
        P(),
        P(),
        P(),
        P(None, "row", "col", None, None),
        P(),
        P(),
    )
    out_specs = P(None, None, "row", "col", None)
    return jax.shard_map(
        per_device, mesh=mesh, in_specs=in_specs, out_specs=out_specs, check_vma=False
    )
```

profile of v0, /device:TPU:1, one launch (start us, length us, event | category | flops | bytes accessed | tf_op | source)
XLA Modules:
  0.0 137.8 jit_solution(3150622637888036031)
XLA Ops:
  0.0 0.0 copy-start
  0.7 0.2 broadcast_multiply_fusion.1
  0.9 3.0 %convolution_bitcast_fusion.1 = f32[1,3,8,16,2,2,16]{6,3,2,1,5,4,0:T(8,128)S(1)} fusion(f32[1,3,8,16,256]{4,3,2,1,0:T(8,128)} %param.8, f32[1,3,8,16,256]{4,3,2,1,0:T(8,128)} %param.9, f32[]{:T(128)} %bitcast.186, f32[1,16,2,256]{3,1,2,0:T(8,128)S(1)} %get-tuple-element.17, f32[1,16,2,256]{3,1,2,0:T(8,128)S(1)} %get-tuple-element.16), kind=kOutput, calls=%fused_computation.16 | convolution fusion | flops 75710464 | bytes 950276 | tf_op jit(solution)/shard_map/bcxyz,rdkz->bcxdrky/dot_general | solution.py:57
  4.0 0.6 copy.77
  4.6 0.6 reshape.643
  5.2 0.8 reshape.645
  6.0 7.6 %all-to-all-start = ((f32[16,1,1536]{2,1,0:T(1,128)}), f32[16,1,1536]{2,1,0:T(1,128)S(1)}, u32[]{:S(2)}, u32[]{:S(2)}) async-start(f32[16,1,1536]{2,1,0:T(1,128)} %reshape.645), calls=%async_computation | async-start | bytes 196608 | tf_op jit(solution)/shard_map/all_to_all | solution.py:60
  13.7 0.0 copy-done.3
  13.7 1.1 fusion.49
  14.8 0.0 copy-start.4
  14.9 0.0 copy-start.5
  14.9 0.3 fusion.69
  15.2 0.1 broadcast_and_fusion.1
  15.3 0.1 broadcast_and_fusion
  15.4 4.9 %all-to-all-done = f32[16,1,1536]{2,1,0:T(1,128)S(1)} async-done(((f32[16,1,1536]{2,1,0:T(1,128)}), f32[16,1,1536]{2,1,0:T(1,128)S(1)}, u32[]{:S(2)}, u32[]{:S(2)}) %all-to-all-start) | async-done | bytes 98336 | tf_op jit(solution)/shard_map/all_to_all | solution.py:60
  20.3 0.6 broadcast.866
  20.9 0.9 reduce
  21.8 0.1 reshape.646
  21.9 0.6 reshape.644
  22.6 4.7 %convolution_bitcast_fusion.4 = f32[1,3,16,2,2,2,8]{2,6,4,1,5,3,0:T(8,128)S(1)} fusion(f32[1,1,16,2,16,16]{5,2,4,0,3,1:T(8,128)S(1)} %get-tuple-element.11, f32[1,1,16,2,16,16]{5,2,4,0,3,1:T(8,128)S(1)} %get-tuple-element.9, f32[1,1,16,2,16,16]{5,2,4,0,3,1:T(8,128)S(1)} %get-tuple-element.10, f32[3,8,16,2,2,16,1,1]{5,4,3,1,0,2,7,6:T(2,128)S(1)} %bitcast.193), kind=kOutput, calls=%fused_computation.20 | convolution fusion | flops 18972672 | bytes 208896 | tf_op jit(solution)/shard_map/bcxsrky,rtdlsy->bcdtklx/dot_general | solution.py:63
  27.2 0.1 copy.32
  27.3 0.8 reduce.1
  28.1 0.7 reshape.647
  28.8 10.5 %all-to-all-start.1 = ((f32[16,1,192]{2,1,0:T(1,128)}), f32[16,1,192]{2,1,0:T(1,128)S(1)}, u32[]{:S(2)}, u32[]{:S(2)}) async-start(f32[16,1,192]{2,1,0:T(1,128)} %reshape.647), calls=%async_computation.1 | async-start | bytes 32768 | tf_op jit(solution)/shard_map/all_to_all | solution.py:65
  39.3 0.1 and_convert_fusion
  39.4 0.8 squeeze.4
  40.2 0.8 squeeze.5
  40.9 5.7 %all-to-all-done.1 = f32[16,1,192]{2,1,0:T(1,128)S(1)} async-done(((f32[16,1,192]{2,1,0:T(1,128)}), f32[16,1,192]{2,1,0:T(1,128)S(1)}, u32[]{:S(2)}, u32[]{:S(2)}) %all-to-all-start.1) | async-done | bytes 12320 | tf_op jit(solution)/shard_map/all_to_all | solution.py:65
  46.7 0.7 reduce.2
  47.4 0.1 reshape.648
  47.5 0.1 copy.33
  47.6 0.6 fusion.10
  48.2 0.4 fusion.8
  48.6 1.7 %fusion.26 = f32[2,32,2,1,32]{4,3,2,1,0:T(1,128)S(1)} fusion(bf16[2,2,32,32,32]{4,3,2,1,0:T(8,128)(2,1)S(1)} %squeeze.4, f32[32,2,32,2,1]{0,2,3,1,4:T(8,128)S(1)} %get-tuple-element.8), kind=kOutput, calls=%fused_computation.40 | convolution fusion | flops 1572864 | bytes 294912 | tf_op jit(solution)/shard_map/lkaoi,bikal->bokal/dot_general | solution.py:91
  50.3 1.7 %fusion.24 = f32[2,32,2,1,32]{4,3,2,1,0:T(1,128)S(1)} fusion(bf16[2,2,32,32,32]{4,3,2,1,0:T(8,128)(2,1)S(1)} %squeeze.4, f32[32,2,32,2,1]{0,2,3,1,4:T(8,128)S(1)} %get-tuple-element.7), kind=kOutput, calls=%fused_computation.38 | convolution fusion | flops 1572864 | bytes 294912 | tf_op jit(solution)/shard_map/lkaoi,bikal->bokal/dot_general | solution.py:91
  52.1 1.7 %fusion.22 = f32[2,32,2,1,32]{4,3,2,1,0:T(1,128)S(1)} fusion(bf16[2,2,32,32,32]{4,3,2,1,0:T(8,128)(2,1)S(1)} %squeeze.5, f32[32,2,32,2,1]{0,2,3,1,4:T(8,128)S(1)} %get-tuple-element.7), kind=kOutput, calls=%fused_computation.36 | convolution fusion | flops 1572864 | bytes 294912 | tf_op jit(solution)/shard_map/lkaoi,bikal->bokal/dot_general | solution.py:91
  53.8 1.7 %fusion.20 = f32[2,32,2,1,32]{4,3,2,1,0:T(1,128)S(1)} fusion(bf16[2,2,32,32,32]{4,3,2,1,0:T(8,128)(2,1)S(1)} %squeeze.5, f32[32,2,32,2,1]{0,2,3,1,4:T(8,128)S(1)} %get-tuple-element.8), kind=kOutput, calls=%fused_computation.34 | convolution fusion | flops 1572864 | bytes 294912 | tf_op jit(solution)/shard_map/lkaoi,bikal->bokal/dot_general | solution.py:91
  55.5 0.1 copy.58
  55.6 0.1 copy.61
  55.7 0.1 copy.62
  55.8 0.1 copy.63
  55.9 0.6 convolution_bitcast_fusion.2
  56.5 0.3 copy.36
  56.8 0.2 copy.37
  57.0 0.2 reshape.649
  57.2 12.0 %all_to_all.20 = f32[16,1,2048]{2,1,0:T(1,128)S(1)} all-to-all(f32[16,1,2048]{2,1,0:T(1,128)S(1)} %reshape.649), channel_id=1, replica_groups=mesh['row'=16,'col'=16] {'row'}, dimensions={0} | all-to-all | bytes 262144 | tf_op jit(solution)/shard_map/all_to_all | solution.py:101
  69.2 1.0 reduce.3
  70.2 0.1 reshape.650
  70.3 0.2 copy.38
  70.5 3.6 %convolution_bitcast_fusion = f32[1,32,16,2,2,8,16]{1,6,5,4,2,3,0:T(8,128)S(1)} fusion(f32[32,16,2,2,2,8,1,1]{0,5,4,3,2,1,7,6:T(8,128)S(1)} %bitcast.190, f32[1,1,16,2,16,16]{5,2,4,0,3,1:T(8,128)S(1)} %get-tuple-element.11, f32[1,1,16,2,16,16]{5,2,4,0,3,1:T(8,128)S(1)} %get-tuple-element.10, f32[1,1,16,2,16,16]{5,2,4,0,3,1:T(8,128)S(1)} %get-tuple-element.9), kind=kOutput, calls=%fused_computation.11 | convolution fusion | flops 201424896 | bytes 1277952 | tf_op jit(solution)/shard_map/bosuklx,uvsldy->bodvkxy/dot_general | solution.py:104
  74.2 2.2 %copy.41 = f32[1,32,16,2,2,8,16]{1,6,5,4,3,2,0:T(8,128)} copy(f32[1,32,16,2,2,8,16]{1,6,5,4,2,3,0:T(8,128)S(1)} %convolution_bitcast_fusion) | data formatting | bytes 2097152 | tf_op jit(solution)/shard_map/bosuklx,uvsldy->bodvkxy/transpose | solution.py:104
  76.4 3.7 %copy.42 = f32[1,32,16,512]{3,1,0,2:T(8,128)} copy(f32[1,32,16,512]{1,3,2,0:T(8,128)} %bitcast.188) | data formatting | bytes 2097152 | tf_op jit(solution)/shard_map/reshape | solution.py:105
  80.1 3.7 %all-to-all-start.3 = ((f32[1,32,16,512]{3,1,0,2:T(8,128)}), f32[1,32,16,512]{3,1,0,2:T(8,128)S(1)}, u32[]{:S(2)}, u32[]{:S(2)}) async-start(f32[1,32,16,512]{3,1,0,2:T(8,128)} %copy.42), calls=%async_computation.3 | async-start | bytes 2097152 | tf_op jit(solution)/shard_map/all_to_all | solution.py:106
  83.8 0.0 copy-done
  83.8 0.1 convolution_bitcast_fusion.6
  83.9 0.1 fusion.11
  84.1 0.0 copy-done.1
  84.1 0.0 copy-done.2
  84.1 0.1 fusion.44
  84.1 5.0 %fusion.30 = f32[8,16,256,32]{2,3,1,0:T(8,128)} fusion(f32[32,3,1,1]{0,1,3,2:T(4,128)S(1)} %convolution_bitcast_fusion.6, f32[3,8,16,256]{3,2,1,0:T(8,128)S(1)} %fusion.44), kind=kOutput, calls=%fused_computation.44 | convolution fusion | flops 37748736 | bytes 4587904 | tf_op jit(solution)/shard_map/oj,bjxyz->boxyz/dot_general | solution.py:118
  89.2 14.5 %all-to-all-done.3 = f32[1,32,16,512]{3,1,0,2:T(8,128)S(1)} async-done(((f32[1,32,16,512]{3,1,0,2:T(8,128)}), f32[1,32,16,512]{3,1,0,2:T(8,128)S(1)}, u32[]{:S(2)}, u32[]{:S(2)}) %all-to-all-start.3) | async-done | bytes 1048608 | tf_op jit(solution)/shard_map/all_to_all | solution.py:106
  103.7 2.6 %copy.43 = f32[1,32,16,512]{1,3,2,0:T(8,128)} copy(f32[1,32,16,512]{3,1,0,2:T(8,128)S(1)} %all-to-all-done.3) | data formatting | bytes 2097152 | tf_op jit(solution)/shard_map/all_to_all | solution.py:106
  106.3 9.1 %copy.44 = f32[32,16,2,2,8,16]{1,5,2,3,4,0:T(8,128)} copy(f32[32,16,2,2,8,16]{0,5,4,3,2,1:T(8,128)} %bitcast.187) | data formatting | bytes 2097152 | tf_op jit(solution)/shard_map/reshape.46
  115.5 22.3 %fusion.7 = bf16[1,32,8,16,256]{4,3,2,1,0:T(8,128)(2,1)} fusion(f32[8,16,256,32]{2,3,1,0:T(8,128)} %fusion.30, f32[32,16,2,2,8,16]{1,5,2,3,4,0:T(8,128)} %copy.44, f32[32]{0:T(128)S(1)} %fusion.11, f32[1,16,2,256]{3,1,2,0:T(8,128)S(1)} %get-tuple-element.18, f32[1,16,2,256]{3,1,2,0:T(8,128)S(1)} %get-tuple-element.15), kind=kOutput, calls=%fused_computation.8 | convolution fusion | flops 816857088 | bytes 7405696 | tf_op jit(solution)/shard_map/bodvkxy,vdkz->boxyz/dot_general | solution.py:114
  (21 shorter events, 0.2 us)
Async XLA Ops:
  0.0 83.8 %copy-start = (f32[32,32]{1,0:T(8,128)S(1)}, f32[32,32]{1,0:T(8,128)}, u32[]{:S(2)}) copy-start(f32[32,32]{1,0:T(8,128)} %param.14) | copy-start | bytes 12292
  0.0 13.7 %copy-start.3 = (bf16[2,2,2,32,1024]{4,3,2,1,0:T(8,128)(2,1)S(1)}, bf16[2,2,2,32,1024]{4,3,2,1,0:T(8,128)(2,1)}, u32[]{:S(2)}) copy-start(bf16[2,2,2,32,1024]{4,3,2,1,0:T(8,128)(2,1)} %param.13) | copy-start | bytes 1572868
  6.0 14.3 %all-to-all-start = ((f32[16,1,1536]{2,1,0:T(1,128)}), f32[16,1,1536]{2,1,0:T(1,128)S(1)}, u32[]{:S(2)}, u32[]{:S(2)}) async-start(f32[16,1,1536]{2,1,0:T(1,128)} %reshape.645), calls=%async_computation | async-start | bytes 196608 | tf_op jit(solution)/shard_map/all_to_all | solution.py:60
  14.8 33.3 %copy-start.4 = (f32[32,3]{0,1:T(4,128)S(1)}, f32[32,3]{0,1:T(4,128)}, u32[]{:S(2)}) copy-start(f32[32,3]{0,1:T(4,128)} %param.11) | copy-start | bytes 1156
  14.9 33.3 %copy-start.5 = (f32[32]{0:T(128)S(1)}, f32[32]{0:T(128)}, u32[]{:S(2)}) copy-start(f32[32]{0:T(128)} %param.12) | copy-start | bytes 388
  28.8 17.9 %all-to-all-start.1 = ((f32[16,1,192]{2,1,0:T(1,128)}), f32[16,1,192]{2,1,0:T(1,128)S(1)}, u32[]{:S(2)}, u32[]{:S(2)}) async-start(f32[16,1,192]{2,1,0:T(1,128)} %reshape.647), calls=%async_computation.1 | async-start | bytes 32768 | tf_op jit(solution)/shard_map/all_to_all | solution.py:65
  76.4 7.5 %copy-start.6 = (f32[32]{0:T(128)S(1)}, f32[32]{0:T(128)}, u32[]{:S(2)}) copy-start(f32[32]{0:T(128)} %param.15) | copy-start | bytes 388
  76.4 7.6 %copy-start.1 = (f32[1,3,8,16,256]{4,3,2,1,0:T(8,128)S(1)}, f32[1,3,8,16,256]{4,3,2,1,0:T(8,128)}, u32[]{:S(2)}) copy-start(f32[1,3,8,16,256]{4,3,2,1,0:T(8,128)} %param.8) | copy-start | bytes 1179652
  76.4 7.6 %copy-start.2 = (f32[1,3,8,16,256]{4,3,2,1,0:T(8,128)S(1)}, f32[1,3,8,16,256]{4,3,2,1,0:T(8,128)}, u32[]{:S(2)}) copy-start(f32[1,3,8,16,256]{4,3,2,1,0:T(8,128)} %param.9) | copy-start | bytes 1179652
  80.1 23.6 %all-to-all-start.3 = ((f32[1,32,16,512]{3,1,0,2:T(8,128)}), f32[1,32,16,512]{3,1,0,2:T(8,128)S(1)}, u32[]{:S(2)}, u32[]{:S(2)}) async-start(f32[1,32,16,512]{3,1,0,2:T(8,128)} %copy.42), calls=%async_computation.3 | async-start | bytes 2097152 | tf_op jit(solution)/shard_map/all_to_all | solution.py:106
where the time goes:
time: 138 us
  matrix products  47.5 us (34%)
  waiting for transfers between devices  25.2 us (18%)
  local copies, waits for them, and re-layouts  24.9 us (18%)
  starting transfers between devices  21.7 us (16%)
  blocking collectives  12 us (9%)
  other arithmetic  5.42 us (4%)
    dot_general x1, matrix products, per_device(): jnp.einsum('bodvkxy,vdkz->boxyz', pencils_z, z_back, precision=highest)  22.3 us
    all_to_all x1, waiting for transfers between devices, per_device(): lax.all_to_all(cells_y, 'col', split_axis=2, concat_axis=2, tiled=True)  14.5 us
    all_to_all x1, blocking collectives, per_device(): lax.all_to_all(cells_x, 'row', split_axis=2, concat_axis=2, tiled=True)  12 us
    all_to_all x1, starting transfers between devices, per_device(): lax.all_to_all(by_y, 'row', split_axis=2, concat_axis=2, tiled=True)  10.5 us
    another operation x3, local copies, waits for them, and re-layouts  9.77 us
    all_to_all x1, starting transfers between devices, per_device(): lax.all_to_all(outgoing, 'col', split_axis=3, concat_axis=3, tiled=True)  7.57 us
    dot_general x4, matrix products, mixing(): jnp.einsum('lkaoi,bikal->bokal', weight_part, data_part, precision=highest)  6.93 us
    all_to_all x1, waiting for transfers between devices, per_device(): lax.all_to_all(by_y, 'row', split_axis=2, concat_axis=2, tiled=True)  5.71 us
  transfers between devices with their start and end apart: 3, of which 3 were waited for; matrix products, arithmetic and copies ran while one was open for 6% of the time, Pallas kernels for 0%

commit v1 on v0

v1 whole, which is shorter than its diff:
```python
import math

import jax
import jax.numpy as jnp
import numpy as np
from jax import lax
from jax.experimental import pallas as pl
from jax.experimental.pallas import tpu as pltpu
from jax.sharding import PartitionSpec as P

NX = 128
NY = 256
NZ = 256
KX = 32
KY = 32
KZ = 32
CH = 32
ROWS = 16
COLS = 16
F32 = jnp.float32
BF16 = jnp.bfloat16


def waves(count):
    index = np.arange(count)
    return np.where(index < count // 2, index, index - count)


def pair(table):
    high = table.astype(np.float32).astype(BF16)
    low = (table - high.astype(np.float64)).astype(np.float32).astype(BF16)
    return high, low


def z_forward():
    angle = 2 * math.pi * ((np.arange(KZ)[:, None] * np.arange(NZ)[None]) % NZ) / NZ
    high, low = pair(np.concatenate([np.cos(angle), -np.sin(angle)], 0))
    return np.concatenate([high, low], 0)


def y_forward():
    angle = 2 * math.pi * ((waves(KY)[:, None] * np.arange(16)[None]) % NY) / NY
    table = np.zeros((8, 16, 2, KY, 8))
    for x in range(8):
        table[x, :, 0, :, x] = np.cos(angle).T
        table[x, :, 1, :, x] = np.sin(angle).T
    high, low = pair(table.reshape(128, 512))
    return np.concatenate([high, high, low], 0)


def y_phase():
    angle = 2 * math.pi * ((waves(KY)[None] * 16 * np.arange(COLS)[:, None]) % NY) / NY
    scale = 1.0 / (NX * NY * NZ)
    table = np.stack([np.cos(angle), np.sin(angle)], 1) * scale
    return np.repeat(table, 8, axis=2).astype(np.float32)


def x_forward():
    angle = 2 * math.pi * ((waves(KX)[None] * np.arange(8)[:, None]) % NX) / NX
    table = np.zeros((4, 2, 2, 8, 2, 3, 2, 2, KX))
    cosine, sine = np.cos(angle), np.sin(angle)
    for c in range(3):
        for e in range(2):
            for d in range(2):
                table[c, 0, e, :, 0, c, e, d] = cosine
                table[c, 1, e, :, 0, c, e, d] = sine
                table[c, 1, e, :, 1, c, e, d] = cosine
                table[c, 0, e, :, 1, c, e, d] = -sine
    high, low = pair(table.reshape(128, 768))
    return np.concatenate([high, high, low], 0)


def x_phase():
    angle = 2 * math.pi * ((waves(KX)[None] * 8 * np.arange(ROWS)[:, None]) % NX) / NX
    table = np.stack([np.cos(angle), np.sin(angle)], 1)
    return np.tile(table, (1, 1, 4)).astype(np.float32)


def x_inverse():
    points = np.arange(NX).reshape(ROWS, 8)
    angle = 2 * math.pi * ((points[:, :, None] * waves(KX)) % NX) / NX
    table = np.zeros((ROWS, 2, 8, 2, KX))
    table[:, 0, :, 0] = np.cos(angle)
    table[:, 0, :, 1] = -np.sin(angle)
    table[:, 1, :, 0] = np.sin(angle)
    table[:, 1, :, 1] = np.cos(angle)
    high, low = pair(table.reshape(256, 64))
    return np.concatenate([high, high, low, low], 1)


def y_inverse():
    angle = 2 * math.pi * ((waves(KY)[:, None] * np.arange(NY)[None]) % NY) / NY
    angle = angle.reshape(ROWS, 2, NY).transpose(1, 0, 2)
    table = np.zeros((2, ROWS, 2, 2, NY))
    table[:, :, 0, 0] = np.cos(angle)
    table[:, :, 1, 0] = -np.sin(angle)
    table[:, :, 0, 1] = np.sin(angle)
    table[:, :, 1, 1] = np.cos(angle)
    high, low = pair(table.reshape(64, 512))
    return np.concatenate([high, high, low, low], 0)


def z_inverse():
    angle = 2 * math.pi * ((np.arange(KZ)[:, None] * np.arange(NZ)[None]) % NZ) / NZ
    double = np.where(np.arange(KZ) == 0, 1.0, 2.0)[:, None]
    angle = angle.reshape(COLS, 2, NZ)
    double = double.reshape(COLS, 2, 1)
    table = np.stack([double * np.cos(angle), -double * np.sin(angle)], 1)
    high, low = pair(table.reshape(64, NZ))
    return np.concatenate([high, high, low, low], 0)


def dot(a, b):
    return jnp.dot(a, b, preferred_element_type=F32)


def dot_t(a, b):
    return lax.dot_general(a, b, (((1,), (1,)), ((), ())), preferred_element_type=F32)


def split(value):
    high = value.astype(BF16)
    low = (value - high.astype(F32)).astype(BF16)
    return high, low


def exchange(arrays, axis, unit):
    arrays = list(arrays)
    length = arrays[0].shape[axis]
    place = lax.broadcasted_iota(jnp.int32, arrays[0].shape, axis)
    bit = 1
    while bit < len(arrays):
        shift = bit * unit
        keep = (place & shift) == 0
        for i in range(len(arrays)):
            if i & bit == 0:
                a, b = arrays[i], arrays[i | bit]
                arrays[i] = jnp.where(keep, a, pltpu.roll(b, shift, axis))
                arrays[i | bit] = jnp.where(keep, pltpu.roll(a, length - shift, axis), b)
        bit *= 2
    return arrays


def forward_kernel(place, step, velocity, tendency, z_table, y_table, phase, advanced, out):
    value = velocity[...] + step[0] * tendency[...]
    advanced[...] = value
    high, low = split(value)
    first = dot_t(z_table[...], high)
    modes = first[:64] + first[64:] + dot_t(z_table[0:64, :], low)
    modes = jnp.concatenate([modes[:, 128 * c : 128 * c + 128] for c in range(3)], 0)
    high, low = split(modes)
    table = y_table[...]
    sums = dot(jnp.concatenate([high, low], 1), table[:256]) + dot(high, table[256:])
    turn = phase[place[1]]
    cosine, sine = turn[0:1], turn[1:2]
    parts = []
    for c in range(3):
        real = sums[64 * c : 64 * c + 32]
        imag = sums[64 * c + 32 : 64 * c + 64]
        re = real[:, :256] + imag[:, 256:]
        im = imag[:, :256] - real[:, 256:]
        parts.append(re * cosine + im * sine)
        parts.append(im * cosine - re * sine)
    zero = jnp.zeros((32, 128), F32)
    for half in range(2):
        lanes = [p[:, 128 * half : 128 * half + 128] for p in parts] + [zero, zero]
        for g, block in enumerate(exchange(lanes, 1, 16)):
            out[8 * half + g] = block


def weight_kernel(weights, lift, out):
    row = lax.broadcasted_iota(jnp.int32, (32, 1024), 0)
    lane = lax.broadcasted_iota(jnp.int32, (32, 1024), 1)
    same = row == lane // 32
    maps = jnp.concatenate([jnp.where(same, lift[j : j + 1, :], 0.0) for j in range(4)], 0)
    high, rest = split(maps)
    rest_f = maps - high.astype(F32)
    mid = rest_f.astype(BF16)
    low = (rest_f - mid.astype(F32)).astype(BF16)
    w = weights[...]
    out[...] = dot_t(high, w) + dot_t(mid, w) + dot_t(low, w)


def mix_kernel(place, arrived, w_eff, x_table, phase, back_table, out):
    sums = []
    for r in range(ROWS):
        block = arrived[r]
        total = (block[0:8] + block[8:16]) + (block[16:24] + block[24:32])
        total = total + pltpu.roll(total, 4, 0)
        total = total + pltpu.roll(total, 2, 0)
        sums.append(total)
    high, low = split(jnp.concatenate(sums, 0))
    table = x_table[...]
    modes = dot(jnp.concatenate([high, low], 1), table[:256]) + dot(high, table[256:])
    real = [None] * 3
    imag = [None] * 3
    for r in range(ROWS):
        cosine, sine = phase[r, 0:1, :], phase[r, 1:2, :]
        for c in range(3):
            re = modes[8 * r : 8 * r + 8, 128 * c : 128 * c + 128]
            im = modes[8 * r : 8 * r + 8, 384 + 128 * c : 512 + 128 * c]
            a = re * cosine + im * sine
            b = im * cosine - re * sine
            real[c] = a if r == 0 else real[c] + a
            imag[c] = b if r == 0 else imag[c] + b
    row = lax.broadcasted_iota(jnp.int32, (8, 128), 0)
    lane = lax.broadcasted_iota(jnp.int32, (8, 128), 1)
    own = ((lane >> 5) & 1) == (row & 1)

    def spread(value):
        value = jnp.where(own, value, pltpu.roll(value, 1, 0))
        return jnp.concatenate([value] * 4, 0)

    weights = w_eff[...]
    mixed_re = None
    for c in range(3):
        cr, ci = spread(real[c]), spread(imag[c])
        wr = weights[32 * c : 32 * c + 32, :128]
        wi = weights[32 * c : 32 * c + 32, 128:]
        a = wr * cr - wi * ci
        b = wr * ci + wi * cr
        mixed_re = a if c == 0 else mixed_re + a
        mixed_im = b if c == 0 else mixed_im + b
    lane = lax.broadcasted_iota(jnp.int32, (32, 128), 1)
    origin = jnp.logical_and(lane == 0, place[0] + place[1] == 0)
    mixed_re = mixed_re + jnp.where(origin, weights[96:128, :128], 0.0)
    mixed_im = mixed_im + jnp.where(origin, weights[96:128, 128:], 0.0)
    turned = jnp.concatenate([mixed_re, mixed_im, mixed_re, mixed_im], 0).T
    blocks = exchange([turned[32 * k : 32 * k + 32] for k in range(4)], 1, 32)
    high, low = split(jnp.concatenate(blocks[:2], 0))
    stack = jnp.concatenate([high, low, high, low], 0)
    out[...] = dot(back_table[...], stack)


def y_kernel(arrived, table, out):
    parts = []
    for group in range(4):
        tiles = [arrived[64 * group + 8 * k : 64 * group + 8 * k + 8, :] for k in range(8)]
        parts.append(exchange(tiles, 0, 1))
    by_x = [jnp.concatenate([parts[g][x] for g in range(4)], 0) for x in range(8)]
    rows = []
    for two in range(4):
        low_ky, high_ky = exchange([by_x[2 * two], by_x[2 * two + 1]], 1, 64)
        data = jnp.concatenate([low_ky, high_ky], 0)
        high = data.astype(BF16).astype(F32)
        rows.append(jnp.concatenate([high, data - high], 0).T.astype(BF16))
    left = jnp.concatenate(rows, 0)
    left = jnp.concatenate([left, left], 1)
    cells = dot(left, table[...])
    for part in range(2):
        for half in range(2):
            lane = 256 * part + 128 * half
            tiles = [cells[64 * x : 64 * x + 64, lane : lane + 128] for x in range(8)]
            for g, block in enumerate(exchange(tiles, 1, 16)):
                out[8 * half + g, 64 * part : 64 * part + 64, :] = block


def local_kernel(combined, advanced, out):
    for o in range(CH):
        out[o] = (
            combined[o, 0] * advanced[0:128, :]
            + combined[o, 1] * advanced[128:256, :]
            + combined[o, 2] * advanced[256:384, :]
            + combined[o, 3]
        )


def z_kernel(arrived, local, table, out):
    block = pl.program_id(0)
    spec = table[...]
    start = pl.multiple_of(block * 8, 8)
    groups = []
    for g in range(8):
        tiles = []
        for k in range(8 * g, 8 * g + 8):
            tiles.append(arrived[k // 4, k % 4, pl.ds(start, 8), :])
        groups.append(exchange(tiles, 0, 1))
    root = math.sqrt(2.0 / math.pi)
    for o in range(8):
        data = jnp.concatenate([groups[g][o] for g in range(8)], 0)
        high = data.astype(BF16).astype(F32)
        left = jnp.concatenate([high, data - high], 0).T.astype(BF16)
        left = jnp.concatenate([left, left], 1)
        value = dot(left, spec) + local[start + o]
        inner = value * (root + (root * 0.044715) * (value * value))
        half = 0.5 * value
        out[o] = (half + half * jnp.tanh(inner)).astype(BF16)


VMEM = pl.BlockSpec(memory_space=pltpu.VMEM)
SMEM = pl.BlockSpec(memory_space=pltpu.SMEM)


def run(kernel, out_shapes, specs, *args, flops=1000000):
    many = isinstance(out_shapes, tuple)
    return pl.pallas_call(
        kernel,
        out_shape=out_shapes,
        in_specs=specs,
        out_specs=tuple(VMEM for _ in out_shapes) if many else VMEM,
        cost_estimate=pl.CostEstimate(flops=flops, transcendentals=0, bytes_accessed=100000),
    )(*args)


def per_device(
    velocity, tendency, step_size, lift_weight, lift_bias, spectral_weight, local_weight, local_bias
):
    highest = lax.Precision.HIGHEST
    place = jnp.stack([lax.axis_index("row"), lax.axis_index("col")]).astype(jnp.int32)
    shape = jax.ShapeDtypeStruct
    advanced, outgoing = run(
        forward_kernel,
        (shape((384, 256), F32), shape((16, 32, 128), F32)),
        [SMEM, SMEM, VMEM, VMEM, VMEM, VMEM, VMEM],
        place,
        step_size,
        velocity.reshape(384, 256),
        tendency.reshape(384, 256),
        z_forward(),
        y_forward(),
        y_phase(),
    )
    arrived = lax.all_to_all(
        outgoing.reshape(256, 2, 128), ("row", "col"), split_axis=0, concat_axis=0, tiled=True
    ).reshape(16, 32, 128)
    lift = jnp.concatenate([lift_weight.T, lift_bias[None]], 0)
    w_eff = run(
        weight_kernel,
        shape((128, 256), F32),
        [VMEM, VMEM],
        spectral_weight.reshape(256, 1024),
        jnp.tile(lift, (1, 32)),
    )
    cells_x = run(
        mix_kernel,
        shape((256, 128), F32),
        [SMEM, VMEM, VMEM, VMEM, VMEM, VMEM],
        place,
        arrived,
        w_eff,
        x_forward(),
        x_phase(),
        x_inverse(),
    )
    by_cells = lax.all_to_all(
        cells_x.reshape(16, 16, 128), "row", split_axis=0, concat_axis=0, tiled=True
    ).reshape(256, 128)
    cells_y = run(y_kernel, shape((16, 128, 128), F32), [VMEM, VMEM], by_cells, y_inverse())
    pencils = lax.all_to_all(cells_y, "col", split_axis=0, concat_axis=0, tiled=True)
    combined = jnp.dot(local_weight, lift_weight, precision=highest)
    offset = jnp.dot(local_weight, lift_bias, precision=highest) + local_bias
    combined = jnp.concatenate([combined, offset[:, None]], 1)
    local = run(local_kernel, shape((32, 128, 256), F32), [SMEM, VMEM], combined, advanced)
    features = pl.pallas_call(
        z_kernel,
        out_shape=shape((32, 128, 256), BF16),
        grid=(4,),
        in_specs=[VMEM, VMEM, VMEM],
        out_specs=pl.BlockSpec((8, 128, 256), lambda i: (i, 0, 0)),
    )(pencils.reshape(16, 4, 32, 128), local, z_inverse())
    return features.reshape(1, 32, 8, 16, 256)


def solution(mesh):
    in_specs = (
        P(None, None, "row", "col", None),
        P(None, None, "row", "col", None),
        P(),
        P(),
        P(),
        P(None, "row", "col", None, None),
        P(),
        P(),
    )
    out_specs = P(None, None, "row", "col", None)
    return jax.shard_map(
        per_device, mesh=mesh, in_specs=in_specs, out_specs=out_specs, check_vma=False
    )
```

time: 138 us -> 85 us (0.62)
  matrix products: 47.5 us -> 0.28 us
  local copies, waits for them, and re-layouts: 24.9 us -> 3.08 us
  Pallas kernels: 0 us -> 20.7 us
  other arithmetic: 5.42 us -> 1.32 us
  starting transfers between devices: 21.7 us -> 19.6 us
    dot_general x12 -> x0, matrix products: 47.2 us -> none  [the longest x1 22.3 us: per_device(): jnp.einsum('bodvkxy,vdkz->boxyz', pencils_z, z_back, precision=highest)]
    pallas_call x0 -> x6, Pallas kernels: none -> 20.7 us  [the longest x5 14.8 us: run(): pl.pallas_call(kernel, out_shape=out_shapes, in_specs=specs, out_specs=tu...]
    another operation x3 -> x2, local copies, waits for them, and re-layouts: 9.77 us -> 0.71 us  [per_device(): jnp.tile(lift, (1, 32))]
    reshape x5 -> x0, local copies, waits for them, and re-layouts: 5.16 us -> none  [the longest x1 3.67 us: per_device(): cells_y = cells_y.reshape(samples, channels, col_count, -1)]
    all_to_all x4 -> x0, local copies, waits for them, and re-layouts: 3.51 us -> none  [the longest x1 2.63 us: per_device(): lax.all_to_all(cells_y, 'col', split_axis=2, concat_axis=2, tiled=True)]
    all_to_all x3 -> x0, other arithmetic: 2.62 us -> none  [the longest x1 0.99 us: per_device(): lax.all_to_all(cells_x, 'row', split_axis=2, concat_axis=2, tiled=True)]
    transpose x3 -> x0, local copies, waits for them, and re-layouts: 2.55 us -> none  [the longest x1 2.24 us: per_device(): jnp.einsum('bosuklx,uvsldy->bodvkxy', by_cells, y_back_table, precision=h...]
    all_to_all x3 -> x2, starting transfers between devices: 21.7 us -> 19.6 us  [the longest x1 15.6 us: per_device(): lax.all_to_all(outgoing.reshape(256, 2, 128), ('row', 'col'), split_axis=...]
  transfers between devices with their start and end apart: 3 -> 2, of which waited for: 3 -> 2; matrix products, arithmetic and copies ran while one was open for 6% -> 3% of each run, Pallas kernels for 0% -> 7%
where the time goes in v1:
time: 85 us; the launch traced here: 84.5 us
  waiting for transfers between devices  26.3 us (31%)
  Pallas kernels  20.7 us (24%)
  starting transfers between devices  19.6 us (23%)
  blocking collectives  12.4 us (15%)
  local copies, waits for them, and re-layouts  3.08 us (4%)
  other arithmetic  1.32 us (2%)
    all_to_all x1, starting transfers between devices, per_device(): lax.all_to_all(outgoing.reshape(256, 2, 128), ('row', 'col'), split_axis=...  15.6 us
    pallas_call x5, Pallas kernels, run(): pl.pallas_call(kernel, out_shape=out_shapes, in_specs=specs, out_specs=tu...  14.8 us
    all_to_all x1, waiting for transfers between devices, per_device(): lax.all_to_all(cells_y, 'col', split_axis=0, concat_axis=0, tiled=True)  14.3 us
    all_to_all x1, blocking collectives, per_device(): lax.all_to_all(cells_x.reshape(16, 16, 128), 'row', split_axis=0, concat_...  12.4 us
    all_to_all x1, waiting for transfers between devices, per_device(): lax.all_to_all(outgoing.reshape(256, 2, 128), ('row', 'col'), split_axis=...  12 us
    pallas_call x1, Pallas kernels, per_device(): pl.pallas_call(z_kernel, out_shape=shape((32, 128, 256), BF16), grid=(4,)...  5.88 us
    all_to_all x1, starting transfers between devices, per_device(): lax.all_to_all(cells_y, 'col', split_axis=0, concat_axis=0, tiled=True)  4 us
  transfers between devices with their start and end apart: 2, of which 2 were waited for; matrix products, arithmetic and copies ran while one was open for 3% of the time, Pallas kernels for 7%

profile of v1, /device:TPU:1, one launch (start us, length us, event | category | flops | bytes accessed | tf_op | source)
XLA Modules:
  0.0 84.5 jit_solution(10409719754498155508)
XLA Ops:
  0.0 0.0 copy-start
  0.0 0.0 copy-start.3
  0.0 0.0 copy-start.4
  0.0 0.0 copy-start.5
  0.7 0.6 pad_add_fusion.place
  1.3 2.7 %shard_map.154 = (f32[384,256]{1,0:T(8,128)}, f32[16,32,128]{2,1,0:T(8,128)}) custom-call(s32[2]{0:T(128)} %pad_add_fusion.place, f32[1]{0:T(128)S(6)} %copy.20.step, f32[384,256]{1,0:T(8,128)} %bitcast.32, f32[384,256]{1,0:T(8,128)} %bitcast.33, bf16[128,256]{1,0:T(8,128)(2,1)} %constant.23.clone.z_table, bf16[384,512]{1,0:T(8,128)(2,1)} %constant.24.clone.y_table, ...), custom_call_target="tpu_custom_call" | custom-call | flops 1000000 | bytes 100000 | tf_op jit(solution)/shard_map/pallas_call | solution.py:296
  4.0 15.6 %all-to-all-start = ((f32[256,2,128]{2,1,0:T(2,128)}), f32[256,2,128]{2,1,0:T(2,128)S(1)}, u32[]{:S(2)}, u32[]{:S(2)}) async-start(f32[256,2,128]{2,1,0:T(2,128)} %bitcast.34), calls=%async_computation | async-start | bytes 524288 | tf_op jit(solution)/shard_map/all_to_all | solution.py:323
  19.7 0.7 pad_maximum_fusion
  20.4 0.7 tile.10.lift
  21.1 2.3 %shard_map.155.w_eff = f32[128,256]{1,0:T(8,128)} custom-call(bf16[256,1024]{1,0:T(8,128)(2,1)} %bitcast.30, f32[4,1024]{1,0:T(4,128)} %tile.10.lift), custom_call_target="tpu_custom_call" | custom-call | flops 1000000 | bytes 100000 | tf_op jit(solution)/shard_map/pallas_call | solution.py:296
  23.4 12.0 %all-to-all-done = f32[256,2,128]{2,1,0:T(2,128)S(1)} async-done(((f32[256,2,128]{2,1,0:T(2,128)}), f32[256,2,128]{2,1,0:T(2,128)S(1)}, u32[]{:S(2)}, u32[]{:S(2)}) %all-to-all-start) | async-done | bytes 262176 | tf_op jit(solution)/shard_map/all_to_all | solution.py:323
  35.4 0.0 copy-start.2
  35.4 0.7 copy-done.2
  36.1 2.7 %shard_map.156 = f32[256,128]{1,0:T(8,128)} custom-call(s32[2]{0:T(128)} %pad_add_fusion.place, f32[16,32,128]{2,1,0:T(8,128)} %bitcast.28, f32[128,256]{1,0:T(8,128)} %shard_map.155.w_eff, bf16[384,768]{1,0:T(8,128)(2,1)} %constant.26.clone.x_table, f32[16,2,128]{2,1,0:T(2,128)} %constant.27.clone.phase, bf16[256,256]{1,0:T(8,128)(2,1)} %constant.28.clone.back_table), custom_call_target="tpu_custom_call" | custom-call | flops 1000000 | bytes 100000 | tf_op jit(solution)/shard_map/pallas_call | solution.py:296
  38.7 12.4 %all_to_all.15 = f32[16,16,128]{2,1,0:T(8,128)} all-to-all(f32[16,16,128]{2,1,0:T(8,128)} %bitcast.29), channel_id=1, replica_groups=mesh['row'=16,'col'=16] {'row'}, dimensions={0} | all-to-all | bytes 262144 | tf_op jit(solution)/shard_map/all_to_all | solution.py:345
  51.2 3.3 %shard_map.157 = f32[16,128,128]{2,1,0:T(8,128)} custom-call(f32[256,128]{1,0:T(8,128)} %bitcast.31, bf16[256,512]{1,0:T(8,128)(2,1)} %constant.29.clone.table), custom_call_target="tpu_custom_call" | custom-call | flops 1000000 | bytes 100000 | tf_op jit(solution)/shard_map/pallas_call | solution.py:296
  54.4 4.0 %all-to-all-start.2 = ((f32[16,128,128]{2,1,0:T(8,128)}), f32[16,128,128]{2,1,0:T(8,128)S(1)}, u32[]{:S(2)}, u32[]{:S(2)}) async-start(f32[16,128,128]{2,1,0:T(8,128)} %shard_map.157), calls=%async_computation.2 | async-start | bytes 2097152 | tf_op jit(solution)/shard_map/all_to_all | solution.py:349
  58.4 0.0 copy-done
  58.5 0.0 copy-done.4
  58.5 0.0 copy-done.5
  58.5 0.1 fusion.1
  58.6 0.0 copy-done.3
  58.6 0.1 fusion.3
  58.8 0.7 copy.19.combined
  59.5 3.9 %shard_map.158.local = f32[32,128,256]{2,1,0:T(8,128)} custom-call(f32[32,4]{1,0:T(8,128)} %copy.19.combined, f32[384,256]{1,0:T(8,128)} %get-tuple-element.8.advanced), custom_call_target="tpu_custom_call" | custom-call | flops 1000000 | bytes 100000 | tf_op jit(solution)/shard_map/pallas_call | solution.py:296
  63.3 14.3 %all-to-all-done.2 = f32[16,128,128]{2,1,0:T(8,128)S(1)} async-done(((f32[16,128,128]{2,1,0:T(8,128)}), f32[16,128,128]{2,1,0:T(8,128)S(1)}, u32[]{:S(2)}, u32[]{:S(2)}) %all-to-all-start.2) | async-done | bytes 1048608 | tf_op jit(solution)/shard_map/all_to_all | solution.py:349
  77.7 0.0 copy-start.1
  77.7 1.0 %copy-done.1 = f32[16,128,128]{2,1,0:T(8,128)} copy-done((f32[16,128,128]{2,1,0:T(8,128)}, f32[16,128,128]{2,1,0:T(8,128)S(1)}, u32[]{:S(2)}) %copy-start.1) | copy-done | bytes 1048600
  78.6 5.9 %shard_map.159 = bf16[32,128,256]{2,1,0:T(8,128)(2,1)} custom-call(f32[16,4,32,128]{3,2,1,0:T(8,128)} %bitcast.27, f32[32,128,256]{2,1,0:T(8,128)} %shard_map.158.local, bf16[256,256]{1,0:T(8,128)(2,1)} %constant.30.clone.table), custom_call_target="tpu_custom_call" | custom-call | tf_op jit(solution)/shard_map/pallas_call | solution.py:354
  (2 shorter events, 0.0 us)
Async XLA Ops:
  0.0 58.4 %copy-start = (f32[32,32]{1,0:T(8,128)S(1)}, f32[32,32]{1,0:T(8,128)}, u32[]{:S(2)}) copy-start(f32[32,32]{1,0:T(8,128)} %param.22) | copy-start | bytes 12292
  0.0 58.6 %copy-start.3 = (f32[32,3]{0,1:T(4,128)S(1)}, f32[32,3]{0,1:T(4,128)}, u32[]{:S(2)}) copy-start(f32[32,3]{0,1:T(4,128)} %param.19) | copy-start | bytes 1156
  0.0 58.5 %copy-start.4 = (f32[32]{0:T(128)S(1)}, f32[32]{0:T(128)}, u32[]{:S(2)}) copy-start(f32[32]{0:T(128)} %param.20) | copy-start | bytes 388
  0.0 58.5 %copy-start.5 = (f32[32]{0:T(128)S(1)}, f32[32]{0:T(128)}, u32[]{:S(2)}) copy-start(f32[32]{0:T(128)} %param.23) | copy-start | bytes 388
  4.0 31.4 %all-to-all-start = ((f32[256,2,128]{2,1,0:T(2,128)}), f32[256,2,128]{2,1,0:T(2,128)S(1)}, u32[]{:S(2)}, u32[]{:S(2)}) async-start(f32[256,2,128]{2,1,0:T(2,128)} %bitcast.34), calls=%async_computation | async-start | bytes 524288 | tf_op jit(solution)/shard_map/all_to_all | solution.py:323
  35.4 0.7 copy-start.2
  54.4 23.2 %all-to-all-start.2 = ((f32[16,128,128]{2,1,0:T(8,128)}), f32[16,128,128]{2,1,0:T(8,128)S(1)}, u32[]{:S(2)}, u32[]{:S(2)}) async-start(f32[16,128,128]{2,1,0:T(8,128)} %shard_map.157), calls=%async_computation.2 | async-start | bytes 2097152 | tf_op jit(solution)/shard_map/all_to_all | solution.py:349
  77.7 1.0 %copy-start.1 = (f32[16,128,128]{2,1,0:T(8,128)}, f32[16,128,128]{2,1,0:T(8,128)S(1)}, u32[]{:S(2)}) copy-start(f32[16,128,128]{2,1,0:T(8,128)S(1)} %all-to-all-done.2) | copy-start | bytes 3145732

commit v2 on v1

--- a/solution.py
+++ b/solution.py
@@ -141,7 +141,7 @@
     return arrays
 
 
-def forward_kernel(place, step, velocity, tendency, z_table, y_table, phase, advanced, out):
+def forward_kernel(step, velocity, tendency, z_table, y_table, phase, advanced, out):
     value = velocity[...] + step[0] * tendency[...]
     advanced[...] = value
     high, low = split(value)
@@ -151,7 +151,7 @@
     high, low = split(modes)
     table = y_table[...]
     sums = dot(jnp.concatenate([high, low], 1), table[:256]) + dot(high, table[256:])
-    turn = phase[place[1]]
+    turn = phase[lax.axis_index("col")]
     cosine, sine = turn[0:1], turn[1:2]
     parts = []
     for c in range(3):
@@ -168,20 +168,66 @@
             out[8 * half + g] = block
 
 
-def weight_kernel(weights, lift, out):
+def prepare_kernel(
+    weights, lift, bias, mixing, mixing_bias, advanced, *rest
+):
+    tables, (w_eff, local), copies, scratch = rest[:5], rest[5:7], rest[7:12], rest[12]
+    for source, target in zip(tables, copies):
+        target[...] = source[...]
+    highest = lax.Precision.HIGHEST
     row = lax.broadcasted_iota(jnp.int32, (32, 1024), 0)
     lane = lax.broadcasted_iota(jnp.int32, (32, 1024), 1)
-    same = row == lane // 32
-    maps = jnp.concatenate([jnp.where(same, lift[j : j + 1, :], 0.0) for j in range(4)], 0)
+    spread = jnp.where(row == (lane & 31), 1.0, 0.0).astype(F32)
+    same = row == (lane >> 5)
+    maps = []
+    for j in range(4):
+        source = lift[j : j + 1, :] if j < 3 else bias[...]
+        source = jnp.broadcast_to(source, (8, 32))
+        wide = jnp.dot(source, spread, precision=highest, preferred_element_type=F32)
+        maps.append(jnp.where(same, wide[0:1, :], 0.0))
+    maps = jnp.concatenate(maps, 0)
     high, rest = split(maps)
-    rest_f = maps - high.astype(F32)
-    mid = rest_f.astype(BF16)
-    low = (rest_f - mid.astype(F32)).astype(BF16)
+    rest = maps - high.astype(F32)
+    mid = rest.astype(BF16)
+    low = (rest - mid.astype(F32)).astype(BF16)
     w = weights[...]
-    out[...] = dot_t(high, w) + dot_t(mid, w) + dot_t(low, w)
-
-
-def mix_kernel(place, arrived, w_eff, x_table, phase, back_table, out):
+    w_eff[...] = dot_t(high, w) + dot_t(mid, w) + dot_t(low, w)
+
+    def columns(matrix, vector):
+        return lax.dot_general(
+            matrix,
+            jnp.broadcast_to(vector, (128, 32)),
+            (((1,), (1,)), ((), ())),
+            precision=highest,
+            preferred_element_type=F32,
+        )
+
+    local_map = mixing[...]
+    eye = jnp.where(
+        lax.broadcasted_iota(jnp.int32, (32, 32), 0) == lax.broadcasted_iota(jnp.int32, (32, 32), 1),
+        1.0,
+        0.0,
+    ).astype(F32)
+    for j in range(3):
+        scratch[j] = columns(local_map, lift[j : j + 1, :])
+    scratch[3] = columns(local_map, bias[...]) + columns(eye, mixing_bias[...])
+
+    def body(o, carry):
+        scale = [scratch[j, pl.ds(o, 1), :] for j in range(4)]
+        for half in range(2):
+            lanes = slice(128 * half, 128 * half + 128)
+            local[o, :, lanes] = (
+                scale[0] * advanced[0:128, lanes]
+                + scale[1] * advanced[128:256, lanes]
+                + scale[2] * advanced[256:384, lanes]
+                + scale[3]
+            )
+        return carry
+
+    lax.fori_loop(0, CH, body, 0)
+
+
+def mix_kernel(arrived, w_eff, x_table, phase, back_table, out):
     sums = []
     for r in range(ROWS):
         block = arrived[r]
@@ -222,7 +268,7 @@
         mixed_re = a if c == 0 else mixed_re + a
         mixed_im = b if c == 0 else mixed_im + b
     lane = lax.broadcasted_iota(jnp.int32, (32, 128), 1)
-    origin = jnp.logical_and(lane == 0, place[0] + place[1] == 0)
+    origin = jnp.logical_and(lane == 0, lax.axis_index("row") + lax.axis_index("col") == 0)
     mixed_re = mixed_re + jnp.where(origin, weights[96:128, :128], 0.0)
     mixed_im = mixed_im + jnp.where(origin, weights[96:128, 128:], 0.0)
     turned = jnp.concatenate([mixed_re, mixed_im, mixed_re, mixed_im], 0).T
@@ -255,16 +301,6 @@
                 out[8 * half + g, 64 * part : 64 * part + 64, :] = block
 
 
-def local_kernel(combined, advanced, out):
-    for o in range(CH):
-        out[o] = (
-            combined[o, 0] * advanced[0:128, :]
-            + combined[o, 1] * advanced[128:256, :]
-            + combined[o, 2] * advanced[256:384, :]
-            + combined[o, 3]
-        )
-
-
 def z_kernel(arrived, local, table, out):
     block = pl.program_id(0)
     spec = table[...]
@@ -291,28 +327,43 @@
 SMEM = pl.BlockSpec(memory_space=pltpu.SMEM)
 
 
-def run(kernel, out_shapes, specs, *args, flops=1000000):
-    many = isinstance(out_shapes, tuple)
+VMEM = "vmem"
+HBM = "hbm"
+SMEM = "smem"
+BLOCKS = {
+    VMEM: pl.BlockSpec(memory_space=pltpu.VMEM),
+    HBM: pl.BlockSpec(memory_space=pltpu.VMEM),
+    SMEM: pl.BlockSpec(memory_space=pltpu.SMEM),
+}
+
+
+def put(value, where):
+    if where == SMEM:
+        return value
+    space = pltpu.VMEM if where == VMEM else pltpu.HBM
+    return pltpu.with_memory_space_constraint(value, space)
+
+
+def run(kernel, outs, specs, *args, scratch=(), limit=16):
     return pl.pallas_call(
         kernel,
-        out_shape=out_shapes,
-        in_specs=specs,
-        out_specs=tuple(VMEM for _ in out_shapes) if many else VMEM,
-        cost_estimate=pl.CostEstimate(flops=flops, transcendentals=0, bytes_accessed=100000),
-    )(*args)
+        out_shape=outs,
+        in_specs=[BLOCKS[s] for s in specs],
+        out_specs=jax.tree.map(lambda _: BLOCKS[VMEM], outs),
+        scratch_shapes=scratch,
+        compiler_params=pltpu.CompilerParams(vmem_limit_bytes=limit * 1024 * 1024),
+        cost_estimate=pl.CostEstimate(flops=1000000, transcendentals=0, bytes_accessed=100000),
+    )(*[put(a, s) for a, s in zip(args, specs)])
 
 
 def per_device(
     velocity, tendency, step_size, lift_weight, lift_bias, spectral_weight, local_weight, local_bias
 ):
-    highest = lax.Precision.HIGHEST
-    place = jnp.stack([lax.axis_index("row"), lax.axis_index("col")]).astype(jnp.int32)
-    shape = jax.ShapeDtypeStruct
+    on_chip = pltpu.VMEM
     advanced, outgoing = run(
         forward_kernel,
-        (shape((384, 256), F32), shape((16, 32, 128), F32)),
-        [SMEM, SMEM, VMEM, VMEM, VMEM, VMEM, VMEM],
-        place,
+        (on_chip((384, 256), F32), on_chip((16, 32, 128), F32)),
+        [SMEM] + [HBM] * 5,
         step_size,
         velocity.reshape(384, 256),
         tendency.reshape(384, 256),
@@ -323,41 +374,44 @@
     arrived = lax.all_to_all(
         outgoing.reshape(256, 2, 128), ("row", "col"), split_axis=0, concat_axis=0, tiled=True
     ).reshape(16, 32, 128)
-    lift = jnp.concatenate([lift_weight.T, lift_bias[None]], 0)
-    w_eff = run(
-        weight_kernel,
-        shape((128, 256), F32),
-        [VMEM, VMEM],
+    tables = [x_forward(), x_phase(), x_inverse(), y_inverse(), z_inverse()]
+    w_eff, local, x_table, turn_table, back_table, y_table, z_table = run(
+        prepare_kernel,
+        [on_chip((128, 256), F32), on_chip((32, 128, 256), F32)]
+        + [on_chip(t.shape, t.dtype) for t in tables],
+        [HBM] * 5 + [VMEM] + [HBM] * 5,
         spectral_weight.reshape(256, 1024),
-        jnp.tile(lift, (1, 32)),
+        lift_weight.T,
+        lift_bias[None],
+        local_weight,
+        local_bias[None],
+        advanced,
+        *tables,
+        scratch=(pltpu.VMEM((4, 32, 128), F32),),
     )
     cells_x = run(
         mix_kernel,
-        shape((256, 128), F32),
-        [SMEM, VMEM, VMEM, VMEM, VMEM, VMEM],
-        place,
+        on_chip((256, 128), F32),
+        [VMEM] * 5,
         arrived,
         w_eff,
-        x_forward(),
-        x_phase(),
-        x_inverse(),
+        x_table,
+        turn_table,
+        back_table,
     )
     by_cells = lax.all_to_all(
         cells_x.reshape(16, 16, 128), "row", split_axis=0, concat_axis=0, tiled=True
     ).reshape(256, 128)
-    cells_y = run(y_kernel, shape((16, 128, 128), F32), [VMEM, VMEM], by_cells, y_inverse())
+    cells_y = run(y_kernel, on_chip((16, 128, 128), F32), [VMEM, VMEM], by_cells, y_table)
     pencils = lax.all_to_all(cells_y, "col", split_axis=0, concat_axis=0, tiled=True)
-    combined = jnp.dot(local_weight, lift_weight, precision=highest)
-    offset = jnp.dot(local_weight, lift_bias, precision=highest) + local_bias
-    combined = jnp.concatenate([combined, offset[:, None]], 1)
-    local = run(local_kernel, shape((32, 128, 256), F32), [SMEM, VMEM], combined, advanced)
     features = pl.pallas_call(
         z_kernel,
-        out_shape=shape((32, 128, 256), BF16),
+        out_shape=jax.ShapeDtypeStruct((32, 128, 256), BF16),
         grid=(4,),
-        in_specs=[VMEM, VMEM, VMEM],
+        in_specs=[BLOCKS[VMEM]] * 3,
         out_specs=pl.BlockSpec((8, 128, 256), lambda i: (i, 0, 0)),
-    )(pencils.reshape(16, 4, 32, 128), local, z_inverse())
+        compiler_params=pltpu.CompilerParams(vmem_limit_bytes=16 * 1024 * 1024),
+    )(put(pencils.reshape(16, 4, 32, 128), VMEM), put(local, VMEM), put(z_table, VMEM))
     return features.reshape(1, 32, 8, 16, 256)
 
 

time: 85 us -> 72.3 us (0.85)
  blocking collectives: 12.4 us -> 31.9 us
  waiting for transfers between devices: 26.3 us -> 9.72 us
  Pallas kernels: 20.7 us -> 12.2 us
  starting transfers between devices: 19.6 us -> 15.6 us
  other arithmetic: 1.32 us -> 0 us
  local copies, waits for them, and re-layouts: 3.08 us -> 1.93 us
    all_to_all x0 -> x1, blocking collectives: none -> 20 us  [per_device(): lax.all_to_all(cells_y, 'col', split_axis=0, concat_axis=0, tiled=True)]
    all_to_all x1 -> x0, waiting for transfers between devices: 14.3 us -> none  [per_device(): lax.all_to_all(cells_y, 'col', split_axis=0, concat_axis=0, tiled=True)]
    pallas_call x6 -> x5, Pallas kernels: 20.7 us -> 12.2 us  [the longest x4 8.78 us: run(): pl.pallas_call(kernel, out_shape=outs, in_specs=[BLOCKS[s] for s in specs...]
    all_to_all x1 -> x0, starting transfers between devices: 4 us -> none  [per_device(): lax.all_to_all(cells_y, 'col', split_axis=0, concat_axis=0, tiled=True)]
    all_to_all x1, waiting for transfers between devices: 12 us -> 9.72 us  [per_device(): lax.all_to_all(outgoing.reshape(256, 2, 128), ('row', 'col'), split_axis=...]
    unnamed x12 -> x4, local copies, waits for them, and re-layouts: 1.68 us -> 1.93 us
  transfers between devices with their start and end apart: 2 -> 1, of which waited for: 2 -> 1; matrix products, arithmetic and copies ran while one was open for 3% -> 0% of each run, Pallas kernels for 7% -> 6%
where the time goes in v2:
time: 72.3 us; the launch traced here: 72 us
  blocking collectives  31.9 us (44%)
  starting transfers between devices  15.6 us (22%)
  Pallas kernels  12.2 us (17%)
  waiting for transfers between devices  9.72 us (13%)
  local copies, waits for them, and re-layouts  1.93 us (3%)
    all_to_all x1, blocking collectives, per_device(): lax.all_to_all(cells_y, 'col', split_axis=0, concat_axis=0, tiled=True)  20 us
    all_to_all x1, starting transfers between devices, per_device(): lax.all_to_all(outgoing.reshape(256, 2, 128), ('row', 'col'), split_axis=...  15.6 us
    all_to_all x1, blocking collectives, per_device(): lax.all_to_all(cells_x.reshape(16, 16, 128), 'row', split_axis=0, concat_...  11.8 us
    all_to_all x1, waiting for transfers between devices, per_device(): lax.all_to_all(outgoing.reshape(256, 2, 128), ('row', 'col'), split_axis=...  9.72 us
    pallas_call x4, Pallas kernels, run(): pl.pallas_call(kernel, out_shape=outs, in_specs=[BLOCKS[s] for s in specs...  8.78 us
    pallas_call x1, Pallas kernels, per_device(): pl.pallas_call(z_kernel, out_shape=jax.ShapeDtypeStruct((32, 128, 256), B...  3.41 us
    unnamed x4, local copies, waits for them, and re-layouts  1.93 us
  transfers between devices with their start and end apart: 1, of which 1 were waited for; matrix products, arithmetic and copies ran while one was open for 0% of the time, Pallas kernels for 6%

profile of v2, /device:TPU:1, one launch (start us, length us, event | category | flops | bytes accessed | tf_op | source)
XLA Modules:
  0.0 72.0 jit_solution(3641871548897175941)
XLA Ops:
  0.7 2.7 %shard_map.154 = (f32[384,256]{1,0:T(8,128)S(1)}, f32[16,32,128]{2,1,0:T(8,128)}) custom-call(f32[1]{0:T(128)S(6)} %copy.17.step, f32[384,256]{1,0:T(8,128)} %bitcast.17, f32[384,256]{1,0:T(8,128)} %bitcast.18, bf16[128,256]{1,0:T(8,128)(2,1)} %constant.16.clone.z_table, bf16[384,512]{1,0:T(8,128)(2,1)} %constant.17.clone.y_table, ...), custom_call_target="tpu_custom_call" | custom-call | flops 1000000 | bytes 100000 | tf_op jit(solution)/shard_map/pallas_call | solution.py:348
  3.4 15.6 %all-to-all-start = ((f32[256,2,128]{2,1,0:T(2,128)}), f32[256,2,128]{2,1,0:T(2,128)S(1)}, u32[]{:S(2)}, u32[]{:S(2)}) async-start(f32[256,2,128]{2,1,0:T(2,128)} %bitcast.2), calls=%async_computation | async-start | bytes 524288 | tf_op jit(solution)/shard_map/all_to_all | solution.py:374
  19.0 4.0 %shard_map.155 = (f32[128,256]{1,0:T(8,128)S(1)}, f32[32,128,256]{2,1,0:T(8,128)S(1)}, bf16[384,768]{1,0:T(8,128)(2,1)S(1)}, f32[16,2,128]{2,1,0:T(2,128)S(1)}, ...) custom-call(bf16[256,1024]{1,0:T(8,128)(2,1)} %bitcast.16, ...), custom_call_target="tpu_custom_call" | custom-call | flops 1000000 | bytes 100000 | tf_op jit(solution)/shard_map/pallas_call | solution.py:348
  23.1 0.0 copy-start
  23.1 1.9 %copy-done = f32[32,128,256]{2,1,0:T(8,128)} copy-done((f32[32,128,256]{2,1,0:T(8,128)}, f32[32,128,256]{2,1,0:T(8,128)S(1)}, u32[]{:S(2)}) %copy-start) | copy-done | bytes 4194328
  25.0 9.7 %all-to-all-done = f32[256,2,128]{2,1,0:T(2,128)S(1)} async-done(((f32[256,2,128]{2,1,0:T(2,128)}), f32[256,2,128]{2,1,0:T(2,128)S(1)}, u32[]{:S(2)}, u32[]{:S(2)}) %all-to-all-start) | async-done | bytes 262176 | tf_op jit(solution)/shard_map/all_to_all | solution.py:374
  34.7 0.0 copy-start.1
  34.7 0.7 %shard_map.156 = f32[256,128]{1,0:T(8,128)S(1)} custom-call(f32[16,32,128]{2,1,0:T(8,128)S(1)} %bitcast.13, f32[128,256]{1,0:T(8,128)S(1)} %get-tuple-element.16.w_eff, bf16[384,768]{1,0:T(8,128)(2,1)S(1)} %get-tuple-element.17.x_table, f32[16,2,128]{2,1,0:T(2,128)S(1)} %get-tuple-element.18.phase, bf16[256,256]{1,0:T(8,128)(2,1)S(1)} %get-tuple-element.19.back_table), custom_call_target="tpu_custom_call" | custom-call | flops 1000000 | bytes 100000 | tf_op jit(solution)/shard_map/pallas_call | solution.py:348
  35.5 11.8 %all_to_all.15 = f32[16,16,128]{2,1,0:T(8,128)S(1)} all-to-all(f32[16,16,128]{2,1,0:T(8,128)S(1)} %bitcast.14), channel_id=1, replica_groups=mesh['row'=16,'col'=16] {'row'}, dimensions={0} | all-to-all | bytes 262144 | tf_op jit(solution)/shard_map/all_to_all | solution.py:402
  47.3 1.3 %shard_map.157 = f32[16,128,128]{2,1,0:T(8,128)S(1)} custom-call(f32[256,128]{1,0:T(8,128)S(1)} %bitcast.15, bf16[256,512]{1,0:T(8,128)(2,1)S(1)} %get-tuple-element.20.table), custom_call_target="tpu_custom_call" | custom-call | flops 1000000 | bytes 100000 | tf_op jit(solution)/shard_map/pallas_call | solution.py:348
  48.6 20.0 %all_to_all.16 = f32[16,128,128]{2,1,0:T(8,128)S(1)} all-to-all(f32[16,128,128]{2,1,0:T(8,128)S(1)} %shard_map.157), channel_id=1, replica_groups=mesh['row'=16,'col'=16] {'col'}, dimensions={0} | all-to-all | bytes 2097152 | tf_op jit(solution)/shard_map/all_to_all | solution.py:406
  68.6 0.0 copy-done.1
  68.6 3.4 %shard_map.158 = bf16[32,128,256]{2,1,0:T(8,128)(2,1)} custom-call(f32[16,4,32,128]{3,2,1,0:T(8,128)S(1)} %bitcast.12, f32[32,128,256]{2,1,0:T(8,128)S(1)} %copy-done.1, bf16[256,256]{1,0:T(8,128)(2,1)S(1)} %get-tuple-element.22.table), custom_call_target="tpu_custom_call" | custom-call | tf_op jit(solution)/shard_map/pallas_call | solution.py:407
Async XLA Ops:
  3.4 31.4 %all-to-all-start = ((f32[256,2,128]{2,1,0:T(2,128)}), f32[256,2,128]{2,1,0:T(2,128)S(1)}, u32[]{:S(2)}, u32[]{:S(2)}) async-start(f32[256,2,128]{2,1,0:T(2,128)} %bitcast.2), calls=%async_computation | async-start | bytes 524288 | tf_op jit(solution)/shard_map/all_to_all | solution.py:374
  23.1 1.9 %copy-start = (f32[32,128,256]{2,1,0:T(8,128)}, f32[32,128,256]{2,1,0:T(8,128)S(1)}, u32[]{:S(2)}) copy-start(f32[32,128,256]{2,1,0:T(8,128)S(1)} %get-tuple-element.21.local) | copy-start | bytes 12582916
  34.7 33.9 %copy-start.1 = (f32[32,128,256]{2,1,0:T(8,128)S(1)}, f32[32,128,256]{2,1,0:T(8,128)}, u32[]{:S(2)}) copy-start(f32[32,128,256]{2,1,0:T(8,128)} %copy-done) | copy-start | bytes 12582916

commit v3 on v2

--- a/solution.py
+++ b/solution.py
@@ -40,12 +40,14 @@
 
 def y_forward():
     angle = 2 * math.pi * ((waves(KY)[:, None] * np.arange(16)[None]) % NY) / NY
-    table = np.zeros((8, 16, 2, KY, 8))
+    table = np.zeros((2, 8, 16, 2, KY, 8))
     for x in range(8):
-        table[x, :, 0, :, x] = np.cos(angle).T
-        table[x, :, 1, :, x] = np.sin(angle).T
-    high, low = pair(table.reshape(128, 512))
-    return np.concatenate([high, high, low], 0)
+        table[0, x, :, 0, :, x] = np.cos(angle).T
+        table[1, x, :, 0, :, x] = np.sin(angle).T
+        table[1, x, :, 1, :, x] = np.cos(angle).T
+        table[0, x, :, 1, :, x] = -np.sin(angle).T
+    high, low = pair(table.reshape(256, 512))
+    return np.concatenate([high, low], 0)
 
 
 def y_phase():
@@ -102,7 +104,7 @@
 
 def z_inverse():
     angle = 2 * math.pi * ((np.arange(KZ)[:, None] * np.arange(NZ)[None]) % NZ) / NZ
-    double = np.where(np.arange(KZ) == 0, 1.0, 2.0)[:, None]
+    double = np.where(np.arange(KZ) == 0, 0.5, 1.0)[:, None]
     angle = angle.reshape(COLS, 2, NZ)
     double = double.reshape(COLS, 2, 1)
     table = np.stack([double * np.cos(angle), -double * np.sin(angle)], 1)
@@ -147,18 +149,19 @@
     high, low = split(value)
     first = dot_t(z_table[...], high)
     modes = first[:64] + first[64:] + dot_t(z_table[0:64, :], low)
-    modes = jnp.concatenate([modes[:, 128 * c : 128 * c + 128] for c in range(3)], 0)
-    high, low = split(modes)
-    table = y_table[...]
-    sums = dot(jnp.concatenate([high, low], 1), table[:256]) + dot(high, table[256:])
+    modes = [
+        jnp.concatenate([modes[0:32, 128 * c : 128 * c + 128], modes[32:64, 128 * c : 128 * c + 128]], 1)
+        for c in range(3)
+    ]
+    high, low = split(jnp.concatenate(modes, 0))
+    first = dot(jnp.concatenate([high, low], 0), y_table[0:256, :])
+    sums = first[:96] + first[96:] + dot(high, y_table[256:512, :])
     turn = phase[lax.axis_index("col")]
     cosine, sine = turn[0:1], turn[1:2]
     parts = []
     for c in range(3):
-        real = sums[64 * c : 64 * c + 32]
-        imag = sums[64 * c + 32 : 64 * c + 64]
-        re = real[:, :256] + imag[:, 256:]
-        im = imag[:, :256] - real[:, 256:]
+        re = sums[32 * c : 32 * c + 32, :256]
+        im = sums[32 * c : 32 * c + 32, 256:]
         parts.append(re * cosine + im * sine)
         parts.append(im * cosine - re * sine)
     zero = jnp.zeros((32, 128), F32)
@@ -168,13 +171,52 @@
             out[8 * half + g] = block
 
 
-def prepare_kernel(
-    weights, lift, bias, mixing, mixing_bias, advanced, *rest
-):
-    tables, (w_eff, local), copies, scratch = rest[:5], rest[5:7], rest[7:12], rest[12]
-    for source, target in zip(tables, copies):
-        target[...] = source[...]
+def prepare_kernel(lift, bias, mixing, mixing_bias, advanced, weights, *rest):
+    tables, (w_eff, local), copies = rest[:5], rest[5:7], rest[7:12]
+    scratch, lines, held_weights, sems = rest[12:]
+    loads = [pltpu.make_async_copy(weights, held_weights, sems.at[0])]
+    for k, (source, target) in enumerate(zip(tables, copies)):
+        loads.append(pltpu.make_async_copy(source, target, sems.at[1 + k]))
+    for load in loads:
+        load.start()
     highest = lax.Precision.HIGHEST
+
+    def columns(matrix, vector):
+        return lax.dot_general(
+            matrix,
+            jnp.broadcast_to(vector, (128, 32)),
+            (((1,), (1,)), ((), ())),
+            precision=highest,
+            preferred_element_type=F32,
+        )
+
+    local_map = mixing[...]
+    eye = jnp.where(
+        lax.broadcasted_iota(jnp.int32, (32, 32), 0) == lax.broadcasted_iota(jnp.int32, (32, 32), 1),
+        1.0,
+        0.0,
+    ).astype(F32)
+    for j in range(3):
+        scratch[j] = 0.5 * columns(local_map, lift[j : j + 1, :])
+    scratch[3] = 0.5 * (columns(local_map, bias[...]) + columns(eye, mixing_bias[...]))
+
+    def body(o, carry):
+        scale = [scratch[j, pl.ds(o, 1), :] for j in range(4)]
+        for half in range(2):
+            lanes = slice(128 * half, 128 * half + 128)
+            lines[o, :, lanes] = (
+                scale[0] * advanced[0:128, lanes]
+                + scale[1] * advanced[128:256, lanes]
+                + scale[2] * advanced[256:384, lanes]
+                + scale[3]
+            )
+        return carry
+
+    for part in range(4):
+        lax.fori_loop(8 * part, 8 * part + 8, body, 0)
+        chunk = pl.ds(8 * part, 8)
+        loads.append(pltpu.make_async_copy(lines.at[chunk], local.at[chunk], sems.at[6 + part]))
+        loads[-1].start()
     row = lax.broadcasted_iota(jnp.int32, (32, 1024), 0)
     lane = lax.broadcasted_iota(jnp.int32, (32, 1024), 1)
     spread = jnp.where(row == (lane & 31), 1.0, 0.0).astype(F32)
@@ -190,41 +232,11 @@
     rest = maps - high.astype(F32)
     mid = rest.astype(BF16)
     low = (rest - mid.astype(F32)).astype(BF16)
-    w = weights[...]
+    loads[0].wait()
+    w = held_weights[...]
     w_eff[...] = dot_t(high, w) + dot_t(mid, w) + dot_t(low, w)
-
-    def columns(matrix, vector):
-        return lax.dot_general(
-            matrix,
-            jnp.broadcast_to(vector, (128, 32)),
-            (((1,), (1,)), ((), ())),
-            precision=highest,
-            preferred_element_type=F32,
-        )
-
-    local_map = mixing[...]
-    eye = jnp.where(
-        lax.broadcasted_iota(jnp.int32, (32, 32), 0) == lax.broadcasted_iota(jnp.int32, (32, 32), 1),
-        1.0,
-        0.0,
-    ).astype(F32)
-    for j in range(3):
-        scratch[j] = columns(local_map, lift[j : j + 1, :])
-    scratch[3] = columns(local_map, bias[...]) + columns(eye, mixing_bias[...])
-
-    def body(o, carry):
-        scale = [scratch[j, pl.ds(o, 1), :] for j in range(4)]
-        for half in range(2):
-            lanes = slice(128 * half, 128 * half + 128)
-            local[o, :, lanes] = (
-                scale[0] * advanced[0:128, lanes]
-                + scale[1] * advanced[128:256, lanes]
-                + scale[2] * advanced[256:384, lanes]
-                + scale[3]
-            )
-        return carry
-
-    lax.fori_loop(0, CH, body, 0)
+    for load in loads[1:]:
+        load.wait()
 
 
 def mix_kernel(arrived, w_eff, x_table, phase, back_table, out):
@@ -301,38 +313,42 @@
                 out[8 * half + g, 64 * part : 64 * part + 64, :] = block
 
 
-def z_kernel(arrived, local, table, out):
-    block = pl.program_id(0)
+def z_kernel(arrived, local, table, out, lines, sems):
     spec = table[...]
-    start = pl.multiple_of(block * 8, 8)
-    groups = []
-    for g in range(8):
-        tiles = []
-        for k in range(8 * g, 8 * g + 8):
-            tiles.append(arrived[k // 4, k % 4, pl.ds(start, 8), :])
-        groups.append(exchange(tiles, 0, 1))
     root = math.sqrt(2.0 / math.pi)
-    for o in range(8):
-        data = jnp.concatenate([groups[g][o] for g in range(8)], 0)
-        high = data.astype(BF16).astype(F32)
-        left = jnp.concatenate([high, data - high], 0).T.astype(BF16)
-        left = jnp.concatenate([left, left], 1)
-        value = dot(left, spec) + local[start + o]
-        inner = value * (root + (root * 0.044715) * (value * value))
-        half = 0.5 * value
-        out[o] = (half + half * jnp.tanh(inner)).astype(BF16)
-
-
-VMEM = pl.BlockSpec(memory_space=pltpu.VMEM)
-SMEM = pl.BlockSpec(memory_space=pltpu.SMEM)
+    stores = []
+    for block in range(4):
+        groups = []
+        for g in range(8):
+            tiles = []
+            for k in range(8 * g, 8 * g + 8):
+                tiles.append(arrived[k // 4, k % 4, 8 * block : 8 * block + 8, :])
+            groups.append(exchange(tiles, 0, 1))
+        for o in range(8):
+            data = jnp.concatenate([groups[g][o] for g in range(8)], 0)
+            high = data.astype(BF16).astype(F32)
+            left = jnp.concatenate([high, data - high], 0).T.astype(BF16)
+            left = jnp.concatenate([left, left], 1)
+            half = dot(left, spec) + local[8 * block + o]
+            inner = half * (2.0 * root + (8.0 * root * 0.044715) * (half * half))
+            lines[8 * block + o] = (half + half * jnp.tanh(inner)).astype(BF16)
+            if o % 4 == 3:
+                chunk = pl.ds(8 * block + o - 3, 4)
+                k = len(stores)
+                stores.append(pltpu.make_async_copy(lines.at[chunk], out.at[chunk], sems.at[k]))
+                stores[-1].start()
+    for store in stores:
+        store.wait()
 
 
 VMEM = "vmem"
 HBM = "hbm"
+ANY = "any"
 SMEM = "smem"
 BLOCKS = {
     VMEM: pl.BlockSpec(memory_space=pltpu.VMEM),
     HBM: pl.BlockSpec(memory_space=pltpu.VMEM),
+    ANY: pl.BlockSpec(memory_space=pl.ANY),
     SMEM: pl.BlockSpec(memory_space=pltpu.SMEM),
 }
 
@@ -344,12 +360,12 @@
     return pltpu.with_memory_space_constraint(value, space)
 
 
-def run(kernel, outs, specs, *args, scratch=(), limit=16):
+def run(kernel, outs, specs, *args, scratch=(), limit=16, out_specs=None):
     return pl.pallas_call(
         kernel,
         out_shape=outs,
         in_specs=[BLOCKS[s] for s in specs],
-        out_specs=jax.tree.map(lambda _: BLOCKS[VMEM], outs),
+        out_specs=jax.tree.map(lambda _: BLOCKS[VMEM], outs) if out_specs is None else [BLOCKS[o] for o in out_specs],
         scratch_shapes=scratch,
         compiler_params=pltpu.CompilerParams(vmem_limit_bytes=limit * 1024 * 1024),
         cost_estimate=pl.CostEstimate(flops=1000000, transcendentals=0, bytes_accessed=100000),
@@ -372,22 +388,28 @@
         y_phase(),
     )
     arrived = lax.all_to_all(
-        outgoing.reshape(256, 2, 128), ("row", "col"), split_axis=0, concat_axis=0, tiled=True
+        outgoing.reshape(256, 1, 256), ("row", "col"), split_axis=0, concat_axis=0, tiled=True
     ).reshape(16, 32, 128)
     tables = [x_forward(), x_phase(), x_inverse(), y_inverse(), z_inverse()]
     w_eff, local, x_table, turn_table, back_table, y_table, z_table = run(
         prepare_kernel,
-        [on_chip((128, 256), F32), on_chip((32, 128, 256), F32)]
+        [on_chip((128, 256), F32), pltpu.HBM((32, 128, 256), F32)]
         + [on_chip(t.shape, t.dtype) for t in tables],
-        [HBM] * 5 + [VMEM] + [HBM] * 5,
-        spectral_weight.reshape(256, 1024),
+        [HBM] * 4 + [VMEM] + [ANY] * 6,
         lift_weight.T,
         lift_bias[None],
         local_weight,
         local_bias[None],
         advanced,
+        spectral_weight.reshape(256, 1024),
         *tables,
-        scratch=(pltpu.VMEM((4, 32, 128), F32),),
+        scratch=(
+            pltpu.VMEM((4, 32, 128), F32),
+            pltpu.VMEM((32, 128, 256), F32),
+            pltpu.VMEM((256, 1024), BF16),
+            pltpu.SemaphoreType.DMA((10,)),
+        ),
+        out_specs=[VMEM, ANY] + [VMEM] * 5,
     )
     cells_x = run(
         mix_kernel,
@@ -404,14 +426,16 @@
     ).reshape(256, 128)
     cells_y = run(y_kernel, on_chip((16, 128, 128), F32), [VMEM, VMEM], by_cells, y_table)
     pencils = lax.all_to_all(cells_y, "col", split_axis=0, concat_axis=0, tiled=True)
-    features = pl.pallas_call(
+    (features,) = run(
         z_kernel,
-        out_shape=jax.ShapeDtypeStruct((32, 128, 256), BF16),
-        grid=(4,),
-        in_specs=[BLOCKS[VMEM]] * 3,
-        out_specs=pl.BlockSpec((8, 128, 256), lambda i: (i, 0, 0)),
-        compiler_params=pltpu.CompilerParams(vmem_limit_bytes=16 * 1024 * 1024),
-    )(put(pencils.reshape(16, 4, 32, 128), VMEM), put(local, VMEM), put(z_table, VMEM))
+        [jax.ShapeDtypeStruct((32, 128, 256), BF16)],
+        [VMEM] * 3,
+        pencils.reshape(16, 4, 32, 128),
+        local,
+        z_table,
+        scratch=(pltpu.VMEM((32, 128, 256), BF16), pltpu.SemaphoreType.DMA((8,))),
+        out_specs=[ANY],
+    )
     return features.reshape(1, 32, 8, 16, 256)
 
 

time: 72.3 us -> 71.5 us (0.989)
  waiting for transfers between devices: 9.72 us -> 11.8 us
  local copies, waits for them, and re-layouts: 1.93 us -> 0.01 us
  Pallas kernels: 12.2 us -> 11.2 us
    pallas_call x1 -> x0, Pallas kernels: 3.41 us -> none  [per_device(): pl.pallas_call(z_kernel, out_shape=jax.ShapeDtypeStruct((32, 128, 256), B...]
    pallas_call x4 -> x5, Pallas kernels: 8.78 us -> 11.2 us  [run(): pl.pallas_call(kernel, out_shape=outs, in_specs=[BLOCKS[s] for s in specs...]
    all_to_all x1, waiting for transfers between devices: 9.72 us -> 11.8 us  [per_device(): lax.all_to_all(outgoing.reshape(256, 1, 256), ('row', 'col'), split_axis=...]
    unnamed x4 -> x2, local copies, waits for them, and re-layouts: 1.93 us -> 0.01 us
  transfers between devices with their start and end apart: 1 -> 1, of which waited for: 1 -> 1; matrix products, arithmetic and copies ran while one was open for 0% -> 0% of each run, Pallas kernels for 6% -> 5%
where the time goes in v3:
time: 71.5 us; the launch traced here: 71.2 us
  blocking collectives  31.9 us (45%)
  starting transfers between devices  15.6 us (22%)
  waiting for transfers between devices  11.8 us (17%)
  Pallas kernels  11.2 us (16%)
    all_to_all x1, blocking collectives, per_device(): lax.all_to_all(cells_y, 'col', split_axis=0, concat_axis=0, tiled=True)  20 us
    all_to_all x1, starting transfers between devices, per_device(): lax.all_to_all(outgoing.reshape(256, 1, 256), ('row', 'col'), split_axis=...  15.6 us
    all_to_all x1, waiting for transfers between devices, per_device(): lax.all_to_all(outgoing.reshape(256, 1, 256), ('row', 'col'), split_axis=...  11.8 us
    all_to_all x1, blocking collectives, per_device(): lax.all_to_all(cells_x.reshape(16, 16, 128), 'row', split_axis=0, concat_...  11.8 us
    pallas_call x5, Pallas kernels, run(): pl.pallas_call(kernel, out_shape=outs, in_specs=[BLOCKS[s] for s in specs...  11.2 us
  transfers between devices with their start and end apart: 1, of which 1 were waited for; matrix products, arithmetic and copies ran while one was open for 0% of the time, Pallas kernels for 5%

profile of v3, /device:TPU:1, one launch (start us, length us, event | category | flops | bytes accessed | tf_op | source)
XLA Modules:
  0.0 71.2 jit_solution(5883273474248301180)
XLA Ops:
  0.7 2.8 %shard_map.154 = (f32[384,256]{1,0:T(8,128)S(1)}, f32[16,32,128]{2,1,0:T(8,128)}) custom-call(f32[1]{0:T(128)S(6)} %copy.18.step, f32[384,256]{1,0:T(8,128)} %bitcast.17, f32[384,256]{1,0:T(8,128)} %bitcast.18, bf16[128,256]{1,0:T(8,128)(2,1)} %constant.16.clone.z_table, bf16[512,512]{1,0:T(8,128)(2,1)} %constant.17.clone.y_table, ...), custom_call_target="tpu_custom_call" | custom-call | flops 1000000 | bytes 100000 | tf_op jit(solution)/shard_map/pallas_call | solution.py:364
  3.4 15.6 %all-to-all-start = ((f32[256,1,256]{2,1,0:T(1,128)}), f32[256,1,256]{2,1,0:T(1,128)S(1)}, u32[]{:S(2)}, u32[]{:S(2)}) async-start(f32[256,1,256]{2,1,0:T(1,128)} %bitcast.2), calls=%async_computation | async-start | bytes 524288 | tf_op jit(solution)/shard_map/all_to_all | solution.py:390
  19.1 3.9 %shard_map.155 = (f32[128,256]{1,0:T(8,128)S(1)}, f32[32,128,256]{2,1,0:T(8,128)}, bf16[384,768]{1,0:T(8,128)(2,1)S(1)}, f32[16,2,128]{2,1,0:T(2,128)S(1)}, bf16...) custom-call(f32[3,32]{1,0:T(4,128)} %bitcast.19, f32[1,32]{1,0:T(1,128)} %bitcast.20, ...), custom_call_target="tpu_custom_call" | custom-call | flops 1000000 | bytes 100000 | tf_op jit(solution)/shard_map/pallas_call | solution.py:364
  22.9 11.8 %all-to-all-done = f32[256,1,256]{2,1,0:T(1,128)S(1)} async-done(((f32[256,1,256]{2,1,0:T(1,128)}), f32[256,1,256]{2,1,0:T(1,128)S(1)}, u32[]{:S(2)}, u32[]{:S(2)}) %all-to-all-start) | async-done | bytes 262176 | tf_op jit(solution)/shard_map/all_to_all | solution.py:390
  34.8 0.0 copy-start
  34.8 0.7 %shard_map.156 = f32[256,128]{1,0:T(8,128)S(1)} custom-call(f32[16,32,128]{2,1,0:T(8,128)S(1)} %bitcast.13, f32[128,256]{1,0:T(8,128)S(1)} %get-tuple-element.16.w_eff, bf16[384,768]{1,0:T(8,128)(2,1)S(1)} %get-tuple-element.17.x_table, f32[16,2,128]{2,1,0:T(2,128)S(1)} %get-tuple-element.18.phase, bf16[256,256]{1,0:T(8,128)(2,1)S(1)} %get-tuple-element.19.back_table), custom_call_target="tpu_custom_call" | custom-call | flops 1000000 | bytes 100000 | tf_op jit(solution)/shard_map/pallas_call | solution.py:364
  35.5 11.8 %all_to_all.15 = f32[16,16,128]{2,1,0:T(8,128)S(1)} all-to-all(f32[16,16,128]{2,1,0:T(8,128)S(1)} %bitcast.14), channel_id=1, replica_groups=mesh['row'=16,'col'=16] {'row'}, dimensions={0} | all-to-all | bytes 262144 | tf_op jit(solution)/shard_map/all_to_all | solution.py:424
  47.3 1.3 %shard_map.157 = f32[16,128,128]{2,1,0:T(8,128)S(1)} custom-call(f32[256,128]{1,0:T(8,128)S(1)} %bitcast.15, bf16[256,512]{1,0:T(8,128)(2,1)S(1)} %get-tuple-element.20.table), custom_call_target="tpu_custom_call" | custom-call | flops 1000000 | bytes 100000 | tf_op jit(solution)/shard_map/pallas_call | solution.py:364
  48.6 20.0 %all_to_all.16 = f32[16,128,128]{2,1,0:T(8,128)S(1)} all-to-all(f32[16,128,128]{2,1,0:T(8,128)S(1)} %shard_map.157), channel_id=1, replica_groups=mesh['row'=16,'col'=16] {'col'}, dimensions={0} | all-to-all | bytes 2097152 | tf_op jit(solution)/shard_map/all_to_all | solution.py:428
  68.6 0.0 copy-done
  68.6 2.6 %shard_map.158 = bf16[32,128,256]{2,1,0:T(8,128)(2,1)} custom-call(f32[16,4,32,128]{3,2,1,0:T(8,128)S(1)} %bitcast.12, f32[32,128,256]{2,1,0:T(8,128)S(1)} %copy-done, bf16[256,256]{1,0:T(8,128)(2,1)S(1)} %get-tuple-element.22.table), custom_call_target="tpu_custom_call" | custom-call | flops 1000000 | bytes 100000 | tf_op jit(solution)/shard_map/pallas_call | solution.py:364
Async XLA Ops:
  3.4 31.4 %all-to-all-start = ((f32[256,1,256]{2,1,0:T(1,128)}), f32[256,1,256]{2,1,0:T(1,128)S(1)}, u32[]{:S(2)}, u32[]{:S(2)}) async-start(f32[256,1,256]{2,1,0:T(1,128)} %bitcast.2), calls=%async_computation | async-start | bytes 524288 | tf_op jit(solution)/shard_map/all_to_all | solution.py:390
  34.8 33.9 %copy-start = (f32[32,128,256]{2,1,0:T(8,128)S(1)}, f32[32,128,256]{2,1,0:T(8,128)}, u32[]{:S(2)}) copy-start(f32[32,128,256]{2,1,0:T(8,128)} %get-tuple-element.21.local) | copy-start | bytes 12582916

commit v4 on v3

--- a/solution.py
+++ b/solution.py
@@ -127,20 +127,16 @@
 
 
 def exchange(arrays, axis, unit):
-    arrays = list(arrays)
-    length = arrays[0].shape[axis]
+    count = len(arrays)
+    length = count * unit
     place = lax.broadcasted_iota(jnp.int32, arrays[0].shape, axis)
+    arrays = [pltpu.roll(a, m * unit, axis) if m else a for m, a in enumerate(arrays)]
     bit = 1
-    while bit < len(arrays):
-        shift = bit * unit
-        keep = (place & shift) == 0
-        for i in range(len(arrays)):
-            if i & bit == 0:
-                a, b = arrays[i], arrays[i | bit]
-                arrays[i] = jnp.where(keep, a, pltpu.roll(b, shift, axis))
-                arrays[i | bit] = jnp.where(keep, pltpu.roll(a, length - shift, axis), b)
+    while bit < count:
+        moved = (place & (bit * unit)) != 0
+        arrays = [jnp.where(moved, arrays[(k + bit) % count], arrays[k]) for k in range(count)]
         bit *= 2
-    return arrays
+    return [arrays[0]] + [pltpu.roll(arrays[count - g], length - g * unit, axis) for g in range(1, count)]
 
 
 def forward_kernel(step, velocity, tendency, z_table, y_table, phase, advanced, out):
@@ -304,11 +300,11 @@
         rows.append(jnp.concatenate([high, data - high], 0).T.astype(BF16))
     left = jnp.concatenate(rows, 0)
     left = jnp.concatenate([left, left], 1)
-    cells = dot(left, table[...])
     for part in range(2):
         for half in range(2):
             lane = 256 * part + 128 * half
-            tiles = [cells[64 * x : 64 * x + 64, lane : lane + 128] for x in range(8)]
+            cells = dot(left, table[:, lane : lane + 128])
+            tiles = [cells[64 * x : 64 * x + 64] for x in range(8)]
             for g, block in enumerate(exchange(tiles, 1, 16)):
                 out[8 * half + g, 64 * part : 64 * part + 64, :] = block
 

time: 71.5 us -> 71.1 us (level)
  no operation moved by 1% of the time
where the time goes in v4:
time: 71.1 us; the launch traced here: 70.8 us
  blocking collectives  31.9 us (45%)
  starting transfers between devices  15.6 us (22%)
  waiting for transfers between devices  11.8 us (17%)
  Pallas kernels  10.8 us (15%)
    all_to_all x1, blocking collectives, per_device(): lax.all_to_all(cells_y, 'col', split_axis=0, concat_axis=0, tiled=True)  20 us
    all_to_all x1, starting transfers between devices, per_device(): lax.all_to_all(outgoing.reshape(256, 1, 256), ('row', 'col'), split_axis=...  15.6 us
    all_to_all x1, waiting for transfers between devices, per_device(): lax.all_to_all(outgoing.reshape(256, 1, 256), ('row', 'col'), split_axis=...  11.8 us
    all_to_all x1, blocking collectives, per_device(): lax.all_to_all(cells_x.reshape(16, 16, 128), 'row', split_axis=0, concat_...  11.8 us
    pallas_call x5, Pallas kernels, run(): pl.pallas_call(kernel, out_shape=outs, in_specs=[BLOCKS[s] for s in specs...  10.8 us
  transfers between devices with their start and end apart: 1, of which 1 were waited for; matrix products, arithmetic and copies ran while one was open for 0% of the time, Pallas kernels for 5%

profile of v4, /device:TPU:1, one launch (start us, length us, event | category | flops | bytes accessed | tf_op | source)
XLA Modules:
  0.0 70.8 jit_solution(10058783094663337109)
XLA Ops:
  0.7 2.7 %shard_map.154 = (f32[384,256]{1,0:T(8,128)S(1)}, f32[16,32,128]{2,1,0:T(8,128)}) custom-call(f32[1]{0:T(128)S(6)} %copy.18.step, f32[384,256]{1,0:T(8,128)} %bitcast.17, f32[384,256]{1,0:T(8,128)} %bitcast.18, bf16[128,256]{1,0:T(8,128)(2,1)} %constant.16.clone.z_table, bf16[512,512]{1,0:T(8,128)(2,1)} %constant.17.clone.y_table, ...), custom_call_target="tpu_custom_call" | custom-call | flops 1000000 | bytes 100000 | tf_op jit(solution)/shard_map/pallas_call | solution.py:360
  3.4 15.6 %all-to-all-start = ((f32[256,1,256]{2,1,0:T(1,128)}), f32[256,1,256]{2,1,0:T(1,128)S(1)}, u32[]{:S(2)}, u32[]{:S(2)}) async-start(f32[256,1,256]{2,1,0:T(1,128)} %bitcast.2), calls=%async_computation | async-start | bytes 524288 | tf_op jit(solution)/shard_map/all_to_all | solution.py:386
  19.0 3.9 %shard_map.155 = (f32[128,256]{1,0:T(8,128)S(1)}, f32[32,128,256]{2,1,0:T(8,128)}, bf16[384,768]{1,0:T(8,128)(2,1)S(1)}, f32[16,2,128]{2,1,0:T(2,128)S(1)}, bf16...) custom-call(f32[3,32]{1,0:T(4,128)} %bitcast.19, f32[1,32]{1,0:T(1,128)} %bitcast.20, ...), custom_call_target="tpu_custom_call" | custom-call | flops 1000000 | bytes 100000 | tf_op jit(solution)/shard_map/pallas_call | solution.py:360
  22.9 11.8 %all-to-all-done = f32[256,1,256]{2,1,0:T(1,128)S(1)} async-done(((f32[256,1,256]{2,1,0:T(1,128)}), f32[256,1,256]{2,1,0:T(1,128)S(1)}, u32[]{:S(2)}, u32[]{:S(2)}) %all-to-all-start) | async-done | bytes 262176 | tf_op jit(solution)/shard_map/all_to_all | solution.py:386
  34.7 0.0 copy-start
  34.7 0.7 %shard_map.156 = f32[256,128]{1,0:T(8,128)S(1)} custom-call(f32[16,32,128]{2,1,0:T(8,128)S(1)} %bitcast.13, f32[128,256]{1,0:T(8,128)S(1)} %get-tuple-element.16.w_eff, bf16[384,768]{1,0:T(8,128)(2,1)S(1)} %get-tuple-element.17.x_table, f32[16,2,128]{2,1,0:T(2,128)S(1)} %get-tuple-element.18.phase, bf16[256,256]{1,0:T(8,128)(2,1)S(1)} %get-tuple-element.19.back_table), custom_call_target="tpu_custom_call" | custom-call | flops 1000000 | bytes 100000 | tf_op jit(solution)/shard_map/pallas_call | solution.py:360
  35.4 11.8 %all_to_all.15 = f32[16,16,128]{2,1,0:T(8,128)S(1)} all-to-all(f32[16,16,128]{2,1,0:T(8,128)S(1)} %bitcast.14), channel_id=1, replica_groups=mesh['row'=16,'col'=16] {'row'}, dimensions={0} | all-to-all | bytes 262144 | tf_op jit(solution)/shard_map/all_to_all | solution.py:420
  47.3 1.0 %shard_map.157 = f32[16,128,128]{2,1,0:T(8,128)S(1)} custom-call(f32[256,128]{1,0:T(8,128)S(1)} %bitcast.15, bf16[256,512]{1,0:T(8,128)(2,1)S(1)} %get-tuple-element.20.table), custom_call_target="tpu_custom_call" | custom-call | flops 1000000 | bytes 100000 | tf_op jit(solution)/shard_map/pallas_call | solution.py:360
  48.3 20.0 %all_to_all.16 = f32[16,128,128]{2,1,0:T(8,128)S(1)} all-to-all(f32[16,128,128]{2,1,0:T(8,128)S(1)} %shard_map.157), channel_id=1, replica_groups=mesh['row'=16,'col'=16] {'col'}, dimensions={0} | all-to-all | bytes 2097152 | tf_op jit(solution)/shard_map/all_to_all | solution.py:424
  68.3 0.0 copy-done
  68.3 2.5 %shard_map.158 = bf16[32,128,256]{2,1,0:T(8,128)(2,1)} custom-call(f32[16,4,32,128]{3,2,1,0:T(8,128)S(1)} %bitcast.12, f32[32,128,256]{2,1,0:T(8,128)S(1)} %copy-done, bf16[256,256]{1,0:T(8,128)(2,1)S(1)} %get-tuple-element.22.table), custom_call_target="tpu_custom_call" | custom-call | flops 1000000 | bytes 100000 | tf_op jit(solution)/shard_map/pallas_call | solution.py:360
Async XLA Ops:
  3.4 31.4 %all-to-all-start = ((f32[256,1,256]{2,1,0:T(1,128)}), f32[256,1,256]{2,1,0:T(1,128)S(1)}, u32[]{:S(2)}, u32[]{:S(2)}) async-start(f32[256,1,256]{2,1,0:T(1,128)} %bitcast.2), calls=%async_computation | async-start | bytes 524288 | tf_op jit(solution)/shard_map/all_to_all | solution.py:386
  34.7 33.6 %copy-start = (f32[32,128,256]{2,1,0:T(8,128)S(1)}, f32[32,128,256]{2,1,0:T(8,128)}, u32[]{:S(2)}) copy-start(f32[32,128,256]{2,1,0:T(8,128)} %get-tuple-element.21.local) | copy-start | bytes 12582916

commit v5 on v4

--- a/solution.py
+++ b/solution.py
@@ -17,6 +17,7 @@
 CH = 32
 ROWS = 16
 COLS = 16
+SNAKE = [4 * i + (j if i % 2 == 0 else 3 - j) for i in range(4) for j in range(4)]
 F32 = jnp.float32
 BF16 = jnp.bfloat16
 
@@ -92,7 +93,7 @@
 
 def y_inverse():
     angle = 2 * math.pi * ((waves(KY)[:, None] * np.arange(NY)[None]) % NY) / NY
-    angle = angle.reshape(ROWS, 2, NY).transpose(1, 0, 2)
+    angle = angle.reshape(ROWS, 2, COLS, 16)[:, :, SNAKE].reshape(ROWS, 2, NY).transpose(1, 0, 2)
     table = np.zeros((2, ROWS, 2, 2, NY))
     table[:, :, 0, 0] = np.cos(angle)
     table[:, :, 1, 0] = -np.sin(angle)
@@ -105,8 +106,8 @@
 def z_inverse():
     angle = 2 * math.pi * ((np.arange(KZ)[:, None] * np.arange(NZ)[None]) % NZ) / NZ
     double = np.where(np.arange(KZ) == 0, 0.5, 1.0)[:, None]
-    angle = angle.reshape(COLS, 2, NZ)
-    double = double.reshape(COLS, 2, 1)
+    angle = angle.reshape(COLS, 2, NZ)[SNAKE]
+    double = double.reshape(COLS, 2, 1)[SNAKE]
     table = np.stack([double * np.cos(angle), -double * np.sin(angle)], 1)
     high, low = pair(table.reshape(64, NZ))
     return np.concatenate([high, high, low, low], 0)
@@ -421,7 +422,9 @@
         cells_x.reshape(16, 16, 128), "row", split_axis=0, concat_axis=0, tiled=True
     ).reshape(256, 128)
     cells_y = run(y_kernel, on_chip((16, 128, 128), F32), [VMEM, VMEM], by_cells, y_table)
-    pencils = lax.all_to_all(cells_y, "col", split_axis=0, concat_axis=0, tiled=True)
+    pencils = lax.all_to_all(
+        cells_y, "col", split_axis=0, concat_axis=0, tiled=True, axis_index_groups=[SNAKE]
+    )
     (features,) = run(
         z_kernel,
         [jax.ShapeDtypeStruct((32, 128, 256), BF16)],

time: 71.1 us -> 69.8 us (0.982)
  blocking collectives: 31.9 us -> 30.6 us
    all_to_all x1, blocking collectives: 20 us -> 18.7 us  [per_device(): lax.all_to_all(cells_y, 'col', split_axis=0, concat_axis=0, tiled=True, a...]
  transfers between devices with their start and end apart: 1 -> 1, of which waited for: 1 -> 1; matrix products, arithmetic and copies ran while one was open for 0% -> 0% of each run, Pallas kernels for 5% -> 6%
where the time goes in v5:
time: 69.8 us; the launch traced here: 69.5 us
  blocking collectives  30.6 us (44%)
  starting transfers between devices  15.6 us (22%)
  waiting for transfers between devices  11.8 us (17%)
  Pallas kernels  10.8 us (15%)
    all_to_all x1, blocking collectives, per_device(): lax.all_to_all(cells_y, 'col', split_axis=0, concat_axis=0, tiled=True, a...  18.7 us
    all_to_all x1, starting transfers between devices, per_device(): lax.all_to_all(outgoing.reshape(256, 1, 256), ('row', 'col'), split_axis=...  15.6 us
    all_to_all x1, waiting for transfers between devices, per_device(): lax.all_to_all(outgoing.reshape(256, 1, 256), ('row', 'col'), split_axis=...  11.8 us
    all_to_all x1, blocking collectives, per_device(): lax.all_to_all(cells_x.reshape(16, 16, 128), 'row', split_axis=0, concat_...  11.8 us
    pallas_call x5, Pallas kernels, run(): pl.pallas_call(kernel, out_shape=outs, in_specs=[BLOCKS[s] for s in specs...  10.8 us
  transfers between devices with their start and end apart: 1, of which 1 were waited for; matrix products, arithmetic and copies ran while one was open for 0% of the time, Pallas kernels for 6%

profile of v5, /device:TPU:1, one launch (start us, length us, event | category | flops | bytes accessed | tf_op | source)
XLA Modules:
  0.0 69.5 jit_solution(15861558124859006617)
XLA Ops:
  0.7 2.7 %shard_map.154 = (f32[384,256]{1,0:T(8,128)S(1)}, f32[16,32,128]{2,1,0:T(8,128)}) custom-call(f32[1]{0:T(128)S(6)} %copy.18.step, f32[384,256]{1,0:T(8,128)} %bitcast.17, f32[384,256]{1,0:T(8,128)} %bitcast.18, bf16[128,256]{1,0:T(8,128)(2,1)} %constant.16.clone.z_table, bf16[512,512]{1,0:T(8,128)(2,1)} %constant.17.clone.y_table, ...), custom_call_target="tpu_custom_call" | custom-call | flops 1000000 | bytes 100000 | tf_op jit(solution)/shard_map/pallas_call | solution.py:361
  3.4 15.6 %all-to-all-start = ((f32[256,1,256]{2,1,0:T(1,128)}), f32[256,1,256]{2,1,0:T(1,128)S(1)}, u32[]{:S(2)}, u32[]{:S(2)}) async-start(f32[256,1,256]{2,1,0:T(1,128)} %bitcast.2), calls=%async_computation | async-start | bytes 524288 | tf_op jit(solution)/shard_map/all_to_all | solution.py:387
  19.0 3.9 %shard_map.155 = (f32[128,256]{1,0:T(8,128)S(1)}, f32[32,128,256]{2,1,0:T(8,128)}, bf16[384,768]{1,0:T(8,128)(2,1)S(1)}, f32[16,2,128]{2,1,0:T(2,128)S(1)}, bf16...) custom-call(f32[3,32]{1,0:T(4,128)} %bitcast.19, f32[1,32]{1,0:T(1,128)} %bitcast.20, ...), custom_call_target="tpu_custom_call" | custom-call | flops 1000000 | bytes 100000 | tf_op jit(solution)/shard_map/pallas_call | solution.py:361
  22.9 11.8 %all-to-all-done = f32[256,1,256]{2,1,0:T(1,128)S(1)} async-done(((f32[256,1,256]{2,1,0:T(1,128)}), f32[256,1,256]{2,1,0:T(1,128)S(1)}, u32[]{:S(2)}, u32[]{:S(2)}) %all-to-all-start) | async-done | bytes 262176 | tf_op jit(solution)/shard_map/all_to_all | solution.py:387
  34.7 0.0 copy-start
  34.7 0.7 %shard_map.156 = f32[256,128]{1,0:T(8,128)S(1)} custom-call(f32[16,32,128]{2,1,0:T(8,128)S(1)} %bitcast.13, f32[128,256]{1,0:T(8,128)S(1)} %get-tuple-element.16.w_eff, bf16[384,768]{1,0:T(8,128)(2,1)S(1)} %get-tuple-element.17.x_table, f32[16,2,128]{2,1,0:T(2,128)S(1)} %get-tuple-element.18.phase, bf16[256,256]{1,0:T(8,128)(2,1)S(1)} %get-tuple-element.19.back_table), custom_call_target="tpu_custom_call" | custom-call | flops 1000000 | bytes 100000 | tf_op jit(solution)/shard_map/pallas_call | solution.py:361
  35.4 11.8 %all_to_all.15 = f32[16,16,128]{2,1,0:T(8,128)S(1)} all-to-all(f32[16,16,128]{2,1,0:T(8,128)S(1)} %bitcast.14), channel_id=1, replica_groups=mesh['row'=16,'col'=16] {'row'}, dimensions={0} | all-to-all | bytes 262144 | tf_op jit(solution)/shard_map/all_to_all | solution.py:421
  47.3 1.0 %shard_map.157 = f32[16,128,128]{2,1,0:T(8,128)S(1)} custom-call(f32[256,128]{1,0:T(8,128)S(1)} %bitcast.15, bf16[256,512]{1,0:T(8,128)(2,1)S(1)} %get-tuple-element.20.table), custom_call_target="tpu_custom_call" | custom-call | flops 1000000 | bytes 100000 | tf_op jit(solution)/shard_map/pallas_call | solution.py:361
  48.3 18.7 %all_to_all.16 = f32[16,128,128]{2,1,0:T(8,128)S(1)} all-to-all(f32[16,128,128]{2,1,0:T(8,128)S(1)} %shard_map.157), channel_id=1, replica_groups={{0,1,2,3,7,6,5,4,8,9,10,11,15,14,13,12},{16,17,18,19,23,22,21,20,24,25,..., dimensions={0} | all-to-all | bytes 2097152 | tf_op jit(solution)/shard_map/all_to_all | solution.py:425
  67.0 0.0 copy-done
  67.0 2.5 %shard_map.158 = bf16[32,128,256]{2,1,0:T(8,128)(2,1)} custom-call(f32[16,4,32,128]{3,2,1,0:T(8,128)S(1)} %bitcast.12, f32[32,128,256]{2,1,0:T(8,128)S(1)} %copy-done, bf16[256,256]{1,0:T(8,128)(2,1)S(1)} %get-tuple-element.22.table), custom_call_target="tpu_custom_call" | custom-call | flops 1000000 | bytes 100000 | tf_op jit(solution)/shard_map/pallas_call | solution.py:361
Async XLA Ops:
  3.4 31.4 %all-to-all-start = ((f32[256,1,256]{2,1,0:T(1,128)}), f32[256,1,256]{2,1,0:T(1,128)S(1)}, u32[]{:S(2)}, u32[]{:S(2)}) async-start(f32[256,1,256]{2,1,0:T(1,128)} %bitcast.2), calls=%async_computation | async-start | bytes 524288 | tf_op jit(solution)/shard_map/all_to_all | solution.py:387
  34.7 32.3 %copy-start = (f32[32,128,256]{2,1,0:T(8,128)S(1)}, f32[32,128,256]{2,1,0:T(8,128)}, u32[]{:S(2)}) copy-start(f32[32,128,256]{2,1,0:T(8,128)} %get-tuple-element.21.local) | copy-start | bytes 12582916

commit v6 on v5

--- a/solution.py
+++ b/solution.py
@@ -18,6 +18,7 @@
 ROWS = 16
 COLS = 16
 SNAKE = [4 * i + (j if i % 2 == 0 else 3 - j) for i in range(4) for j in range(4)]
+CHAIN = [2 * z for z in range(8)] + [2 * z + 1 for z in range(7, -1, -1)]
 F32 = jnp.float32
 BF16 = jnp.bfloat16
 
@@ -80,7 +81,7 @@
 
 
 def x_inverse():
-    points = np.arange(NX).reshape(ROWS, 8)
+    points = np.arange(NX).reshape(ROWS, 8)[CHAIN]
     angle = 2 * math.pi * ((points[:, :, None] * waves(KX)) % NX) / NX
     table = np.zeros((ROWS, 2, 8, 2, KX))
     table[:, 0, :, 0] = np.cos(angle)
@@ -93,7 +94,7 @@
 
 def y_inverse():
     angle = 2 * math.pi * ((waves(KY)[:, None] * np.arange(NY)[None]) % NY) / NY
-    angle = angle.reshape(ROWS, 2, COLS, 16)[:, :, SNAKE].reshape(ROWS, 2, NY).transpose(1, 0, 2)
+    angle = angle.reshape(ROWS, 2, COLS, 16)[CHAIN][:, :, SNAKE].reshape(ROWS, 2, NY).transpose(1, 0, 2)
     table = np.zeros((2, ROWS, 2, 2, NY))
     table[:, :, 0, 0] = np.cos(angle)
     table[:, :, 1, 0] = -np.sin(angle)
@@ -419,7 +420,7 @@
         back_table,
     )
     by_cells = lax.all_to_all(
-        cells_x.reshape(16, 16, 128), "row", split_axis=0, concat_axis=0, tiled=True
+        cells_x.reshape(16, 16, 128), "row", split_axis=0, concat_axis=0, tiled=True, axis_index_groups=[CHAIN]
     ).reshape(256, 128)
     cells_y = run(y_kernel, on_chip((16, 128, 128), F32), [VMEM, VMEM], by_cells, y_table)
     pencils = lax.all_to_all(

time: 69.8 us -> 69.8 us (level)
  no operation moved by 1% of the time
where the time goes in v6:
time: 69.8 us; the launch traced here: 69.5 us
  blocking collectives  30.5 us (44%)
  starting transfers between devices  15.6 us (22%)
  waiting for transfers between devices  11.8 us (17%)
  Pallas kernels  10.8 us (15%)
    all_to_all x1, blocking collectives, per_device(): lax.all_to_all(cells_y, 'col', split_axis=0, concat_axis=0, tiled=True, a...  18.6 us
    all_to_all x1, starting transfers between devices, per_device(): lax.all_to_all(outgoing.reshape(256, 1, 256), ('row', 'col'), split_axis=...  15.6 us
    all_to_all x1, blocking collectives, per_device(): lax.all_to_all(cells_x.reshape(16, 16, 128), 'row', split_axis=0, concat_...  12 us
    all_to_all x1, waiting for transfers between devices, per_device(): lax.all_to_all(outgoing.reshape(256, 1, 256), ('row', 'col'), split_axis=...  11.8 us
    pallas_call x5, Pallas kernels, run(): pl.pallas_call(kernel, out_shape=outs, in_specs=[BLOCKS[s] for s in specs...  10.8 us
  transfers between devices with their start and end apart: 1, of which 1 were waited for; matrix products, arithmetic and copies ran while one was open for 0% of the time, Pallas kernels for 6%

profile of v6, /device:TPU:1, one launch (start us, length us, event | category | flops | bytes accessed | tf_op | source)
XLA Modules:
  0.0 69.5 jit_solution(6063891652429303170)
XLA Ops:
  0.7 2.7 %shard_map.154 = (f32[384,256]{1,0:T(8,128)S(1)}, f32[16,32,128]{2,1,0:T(8,128)}) custom-call(f32[1]{0:T(128)S(6)} %copy.18.step, f32[384,256]{1,0:T(8,128)} %bitcast.17, f32[384,256]{1,0:T(8,128)} %bitcast.18, bf16[128,256]{1,0:T(8,128)(2,1)} %constant.16.clone.z_table, bf16[512,512]{1,0:T(8,128)(2,1)} %constant.17.clone.y_table, ...), custom_call_target="tpu_custom_call" | custom-call | flops 1000000 | bytes 100000 | tf_op jit(solution)/shard_map/pallas_call | solution.py:362
  3.4 15.6 %all-to-all-start = ((f32[256,1,256]{2,1,0:T(1,128)}), f32[256,1,256]{2,1,0:T(1,128)S(1)}, u32[]{:S(2)}, u32[]{:S(2)}) async-start(f32[256,1,256]{2,1,0:T(1,128)} %bitcast.2), calls=%async_computation | async-start | bytes 524288 | tf_op jit(solution)/shard_map/all_to_all | solution.py:388
  19.0 3.9 %shard_map.155 = (f32[128,256]{1,0:T(8,128)S(1)}, f32[32,128,256]{2,1,0:T(8,128)}, bf16[384,768]{1,0:T(8,128)(2,1)S(1)}, f32[16,2,128]{2,1,0:T(2,128)S(1)}, bf16...) custom-call(f32[3,32]{1,0:T(4,128)} %bitcast.19, f32[1,32]{1,0:T(1,128)} %bitcast.20, ...), custom_call_target="tpu_custom_call" | custom-call | flops 1000000 | bytes 100000 | tf_op jit(solution)/shard_map/pallas_call | solution.py:362
  22.9 11.8 %all-to-all-done = f32[256,1,256]{2,1,0:T(1,128)S(1)} async-done(((f32[256,1,256]{2,1,0:T(1,128)}), f32[256,1,256]{2,1,0:T(1,128)S(1)}, u32[]{:S(2)}, u32[]{:S(2)}) %all-to-all-start) | async-done | bytes 262176 | tf_op jit(solution)/shard_map/all_to_all | solution.py:388
  34.7 0.0 copy-start
  34.7 0.7 %shard_map.156 = f32[256,128]{1,0:T(8,128)S(1)} custom-call(f32[16,32,128]{2,1,0:T(8,128)S(1)} %bitcast.13, f32[128,256]{1,0:T(8,128)S(1)} %get-tuple-element.16.w_eff, bf16[384,768]{1,0:T(8,128)(2,1)S(1)} %get-tuple-element.17.x_table, f32[16,2,128]{2,1,0:T(2,128)S(1)} %get-tuple-element.18.phase, bf16[256,256]{1,0:T(8,128)(2,1)S(1)} %get-tuple-element.19.back_table), custom_call_target="tpu_custom_call" | custom-call | flops 1000000 | bytes 100000 | tf_op jit(solution)/shard_map/pallas_call | solution.py:362
  35.4 12.0 %all_to_all.15 = f32[16,16,128]{2,1,0:T(8,128)S(1)} all-to-all(f32[16,16,128]{2,1,0:T(8,128)S(1)} %bitcast.14), channel_id=1, replica_groups={{0,32,64,96,128,160,192,224,240,208,176,144,112,80,48,16},{1,33,65,97,1..., dimensions={0} | all-to-all | bytes 262144 | tf_op jit(solution)/shard_map/all_to_all | solution.py:422
  47.4 1.0 %shard_map.157 = f32[16,128,128]{2,1,0:T(8,128)S(1)} custom-call(f32[256,128]{1,0:T(8,128)S(1)} %bitcast.15, bf16[256,512]{1,0:T(8,128)(2,1)S(1)} %get-tuple-element.20.table), custom_call_target="tpu_custom_call" | custom-call | flops 1000000 | bytes 100000 | tf_op jit(solution)/shard_map/pallas_call | solution.py:362
  48.4 18.6 %all_to_all.16 = f32[16,128,128]{2,1,0:T(8,128)S(1)} all-to-all(f32[16,128,128]{2,1,0:T(8,128)S(1)} %shard_map.157), channel_id=1, replica_groups={{0,1,2,3,7,6,5,4,8,9,10,11,15,14,13,12},{16,17,18,19,23,22,21,20,24,25,..., dimensions={0} | all-to-all | bytes 2097152 | tf_op jit(solution)/shard_map/all_to_all | solution.py:426
  67.0 0.0 copy-done
  67.0 2.5 %shard_map.158 = bf16[32,128,256]{2,1,0:T(8,128)(2,1)} custom-call(f32[16,4,32,128]{3,2,1,0:T(8,128)S(1)} %bitcast.12, f32[32,128,256]{2,1,0:T(8,128)S(1)} %copy-done, bf16[256,256]{1,0:T(8,128)(2,1)S(1)} %get-tuple-element.22.table), custom_call_target="tpu_custom_call" | custom-call | flops 1000000 | bytes 100000 | tf_op jit(solution)/shard_map/pallas_call | solution.py:362
Async XLA Ops:
  3.4 31.4 %all-to-all-start = ((f32[256,1,256]{2,1,0:T(1,128)}), f32[256,1,256]{2,1,0:T(1,128)S(1)}, u32[]{:S(2)}, u32[]{:S(2)}) async-start(f32[256,1,256]{2,1,0:T(1,128)} %bitcast.2), calls=%async_computation | async-start | bytes 524288 | tf_op jit(solution)/shard_map/all_to_all | solution.py:388
  34.7 32.3 %copy-start = (f32[32,128,256]{2,1,0:T(8,128)S(1)}, f32[32,128,256]{2,1,0:T(8,128)}, u32[]{:S(2)}) copy-start(f32[32,128,256]{2,1,0:T(8,128)} %get-tuple-element.21.local) | copy-start | bytes 12582916
